TPU v7x, 512 devices: a whole 4x8x8 slice. The times are simulated.
512 devices in a mesh: tm: 256 (over z, y, x), chan: 2 (over core).
Axes of the slice: x: 4, y: 8, z: 8, core: 2. Of those that a mesh axis runs over, the one named last changes fastest.
Arguments:
- signal: bfloat16 [3, 32768, 512], P(None, 'tm', 'chan'), may hold values from -6 to 6
- taps: float32 [10, 2, 512], P(None, None, 'chan'), may hold values from -3 to 3
- w_gate: bfloat16 [10, 512, 2, 512], P(None, None, None, 'chan'), may hold values from -0.25 to 0.25
- w_res: bfloat16 [10, 512, 512], P(None, None, 'chan'), may hold values from -0.25 to 0.25
- w_skip: bfloat16 [10, 512, 512], P(None, None, 'chan'), may hold values from -0.1875 to 0.1875
Outputs:
- stream: bfloat16 [3, 32768, 512], P(None, 'tm', 'chan')
- skips: bfloat16 [3, 32768, 512], P(None, 'tm', 'chan')
All inputs are finite; a program needn't handle non-finite values.
Results may differ from a plain program's by a relative error of at most 0.02.
Values may be sent and summed in bfloat16 or wider, within the bound.
No kernel may reach another device: no remote copies, remote signals or barrier semaphores. Data moves between devices by JAX's collectives and lax.ppermute only.
A program may use at most 64 MiB of HBM per device.

v0:
```python
import jax
import jax.numpy as jnp
from jax import lax
from jax.sharding import PartitionSpec as P

LAYERS = 10


def shifted(value, axis, steps):
    count = lax.axis_size(axis)
    leading, last = (max(0, -steps), min(count, count - steps))
    return lax.ppermute(value, axis, [(source, source + steps) for source in range(leading, last)])


def delay_block(stream, delay, near_fn, far_fn):
    length = stream.shape[1]
    whole, rest = divmod(delay, length)
    if whole == 0:
        nearer = stream
    else:
        nearer = near_fn(stream, whole)
    if rest == 0:
        return nearer
    farther = far_fn(stream[:, length - rest :], whole + 1)
    return jnp.concatenate([farther, nearer[:, : length - rest]], axis=1)


def near_time(block, steps):
    return shifted(block, "tm", steps)


def far_time(block, steps):
    return shifted(block, "tm", steps)


def gate_units(hidden):
    return (jnp.tanh(hidden[:, :, 0]) * jax.nn.sigmoid(hidden[:, :, 1])).astype(jnp.bfloat16)


def local(signal, taps, w_gate, w_res, w_skip):
    stream = signal
    seqs, length, local_c = stream.shape
    skip = jnp.zeros((seqs, length, local_c), jnp.float32)
    for layer in range(LAYERS):
        delayed = delay_block(stream, 2**layer, near_time, far_time)
        conv = (
            taps[layer, 0] * delayed.astype(jnp.float32)
            + taps[layer, 1] * stream.astype(jnp.float32)
        ).astype(jnp.bfloat16)
        gate_w = w_gate[layer]
        hidden = jnp.einsum(
            "stc,cko->stko",
            lax.all_gather(conv, "chan", axis=2, tiled=True),
            gate_w,
            preferred_element_type=jnp.float32,
        )
        gated = gate_units(hidden)
        res_w = w_res[layer]
        skip_w = w_skip[layer]
        piece = lax.all_gather(gated, "chan", axis=2, tiled=True)
        update = jnp.einsum("stc,co->sto", piece, res_w, preferred_element_type=jnp.float32)
        skip_part = jnp.einsum("stc,co->sto", piece, skip_w, preferred_element_type=jnp.float32)
        stream = (stream.astype(jnp.float32) + update).astype(jnp.bfloat16)
        skip = skip + skip_part
    return (stream, skip.astype(jnp.bfloat16))


def solution(mesh):
    in_specs = (
        P(None, "tm", "chan"),
        P(None, None, "chan"),
        P(None, None, None, "chan"),
        P(None, None, "chan"),
        P(None, None, "chan"),
    )
    out_specs = (P(None, "tm", "chan"), P(None, "tm", "chan"))
    return jax.shard_map(local, mesh=mesh, in_specs=in_specs, out_specs=out_specs, check_vma=False)
```

profile of v0, /device:TPU:257, one launch (start us, length us, event | category | flops | bytes accessed | tf_op | source)
XLA Modules:
  0.0 173.9 jit_solution(2866899090610819698)
XLA Ops:
  1.4 3.3 %collective-permute-start = (bf16[3,1,256]{2,1,0:T(2,128)(2,1)S(1)}, bf16[3,1,256]{2,1,0:T(2,128)(2,1)S(1)}, u32[]{:S(2)}, u32[]{:S(2)}) collective-permute-start(bf16[3,1,256]{2,1,0:T(2,128)(2,1)S(1)} %slice.253), channel_id=1, source_target_pairs={{0,2},{2,4},{4,6},{6,8},{8,10},{10,12},{12,14},{14,16},{16,18},{18... | collective-permute-start | bytes 4616 | tf_op jit(solution)/shard_map/ppermute | solution.py:12
  4.6 6.0 %fusion.162 = (bf16[1,512,2,256]{3,2,1,0:T(2,128)(2,1)S(1)}, bf16[1,512,2,256]{3,2,1,0:T(2,128)(2,1)S(1)}, bf16[1,512,2,256]{3,2,1,0:T(2,128)(2,1)S(1)}, bf16[1,...) fusion(bf16[10,512,2,256]{3,2,1,0:T(2,128)(2,1)} %param.7), kind=kLoop, calls=%fused_computation.221 | loop fusion | bytes 10485760 | tf_op jit(solution)/shard_map/slice | solution.py:50
  11.4 3.7 %all_gather.60 = bf16[3,128,512]{2,1,0:T(8,128)(2,1)S(1)} all-gather(bf16[3,128,256]{2,1,0:T(8,128)(2,1)S(1)} %fusion.22), channel_id=1, replica_groups=mesh['tm'=256,'chan'=2] {'chan'}, dimensions={2}, use_global_device_ids=true | all-gather | bytes 589824 | tf_op jit(solution)/shard_map/all_gather | solution.py:53
  15.6 2.1 %all-gather = bf16[3,128,1,512]{3,1,2,0:T(8,128)(2,1)S(1)} all-gather(bf16[3,128,1,256]{3,1,2,0:T(8,128)(2,1)S(1)} %fusion.112), channel_id=2, replica_groups=mesh['tm'=256,'chan'=2] {'chan'}, dimensions={3}, use_global_device_ids=true | all-gather | bytes 589824 | tf_op jit(solution)/shard_map/all_gather | solution.py:60
  20.2 7.6 %collective-permute-done.1 = bf16[3,2,256]{2,1,0:T(2,128)(2,1)S(1)} collective-permute-done((bf16[3,2,256]{2,1,0:T(2,128)(2,1)S(1)}, bf16[3,2,256]{2,1,0:T(2,128)(2,1)S(1)}, u32[]{:S(2)}, u32[]{:S(2)}) %collective-permute-start.1) | collective-permute-done | bytes 3104 | tf_op jit(solution)/shard_map/ppermute | solution.py:12
  27.8 3.2 %all_gather.62 = bf16[3,128,512]{2,1,0:T(8,128)(2,1)S(1)} all-gather(bf16[3,128,256]{2,1,0:T(8,128)(2,1)S(1)} %fusion.24), channel_id=1, replica_groups=mesh['tm'=256,'chan'=2] {'chan'}, dimensions={2}, use_global_device_ids=true | all-gather | bytes 589824 | tf_op jit(solution)/shard_map/all_gather | solution.py:53
  36.2 7.6 %collective-permute-done.2 = bf16[3,4,256]{2,1,0:T(4,128)(2,1)S(1)} collective-permute-done((bf16[3,4,256]{2,1,0:T(4,128)(2,1)S(1)}, bf16[3,4,256]{2,1,0:T(4,128)(2,1)S(1)}, u32[]{:S(2)}, u32[]{:S(2)}) %collective-permute-start.2) | collective-permute-done | bytes 6176 | tf_op jit(solution)/shard_map/ppermute | solution.py:12
  43.9 3.2 %all_gather.64 = bf16[3,128,512]{2,1,0:T(8,128)(2,1)S(1)} all-gather(bf16[3,128,256]{2,1,0:T(8,128)(2,1)S(1)} %fusion.26), channel_id=1, replica_groups=mesh['tm'=256,'chan'=2] {'chan'}, dimensions={2}, use_global_device_ids=true | all-gather | bytes 589824 | tf_op jit(solution)/shard_map/all_gather | solution.py:53
  52.3 7.6 %collective-permute-done.3 = bf16[3,8,256]{2,1,0:T(8,128)(2,1)S(1)} collective-permute-done((bf16[3,8,256]{2,1,0:T(8,128)(2,1)S(1)}, bf16[3,8,256]{2,1,0:T(8,128)(2,1)S(1)}, u32[]{:S(2)}, u32[]{:S(2)}) %collective-permute-start.3) | collective-permute-done | bytes 12320 | tf_op jit(solution)/shard_map/ppermute | solution.py:12
  60.0 3.2 %all_gather.66 = bf16[3,128,512]{2,1,0:T(8,128)(2,1)S(1)} all-gather(bf16[3,128,256]{2,1,0:T(8,128)(2,1)S(1)} %fusion.28), channel_id=1, replica_groups=mesh['tm'=256,'chan'=2] {'chan'}, dimensions={2}, use_global_device_ids=true | all-gather | bytes 589824 | tf_op jit(solution)/shard_map/all_gather | solution.py:53
  68.4 7.8 %collective-permute-done.4 = bf16[3,16,256]{2,1,0:T(8,128)(2,1)S(1)} collective-permute-done((bf16[3,16,256]{2,1,0:T(8,128)(2,1)S(1)}, bf16[3,16,256]{2,1,0:T(8,128)(2,1)S(1)}, u32[]{:S(2)}, u32[]{:S(2)}) %collective-permute-start.4) | collective-permute-done | bytes 24608 | tf_op jit(solution)/shard_map/ppermute | solution.py:12
  76.2 3.2 %all_gather.68 = bf16[3,128,512]{2,1,0:T(8,128)(2,1)S(1)} all-gather(bf16[3,128,256]{2,1,0:T(8,128)(2,1)S(1)} %fusion.30), channel_id=1, replica_groups=mesh['tm'=256,'chan'=2] {'chan'}, dimensions={2}, use_global_device_ids=true | all-gather | bytes 589824 | tf_op jit(solution)/shard_map/all_gather | solution.py:53
  80.0 2.1 %all-gather.4 = bf16[3,128,1,512]{3,1,2,0:T(8,128)(2,1)S(1)} all-gather(bf16[3,128,1,256]{3,1,2,0:T(8,128)(2,1)S(1)} %fusion.116), channel_id=6, replica_groups=mesh['tm'=256,'chan'=2] {'chan'}, dimensions={3}, use_global_device_ids=true | all-gather | bytes 589824 | tf_op jit(solution)/shard_map/all_gather | solution.py:60
  84.6 8.0 %collective-permute-done.5 = bf16[3,32,256]{2,1,0:T(8,128)(2,1)S(1)} collective-permute-done((bf16[3,32,256]{2,1,0:T(8,128)(2,1)S(1)}, bf16[3,32,256]{2,1,0:T(8,128)(2,1)S(1)}, u32[]{:S(2)}, u32[]{:S(2)}) %collective-permute-start.5) | collective-permute-done | bytes 49184 | tf_op jit(solution)/shard_map/ppermute | solution.py:12
  92.7 3.2 %all_gather.70 = bf16[3,128,512]{2,1,0:T(8,128)(2,1)S(1)} all-gather(bf16[3,128,256]{2,1,0:T(8,128)(2,1)S(1)} %fusion.32), channel_id=1, replica_groups=mesh['tm'=256,'chan'=2] {'chan'}, dimensions={2}, use_global_device_ids=true | all-gather | bytes 589824 | tf_op jit(solution)/shard_map/all_gather | solution.py:53
  101.1 9.1 %collective-permute-done.6 = bf16[3,64,256]{2,1,0:T(8,128)(2,1)S(1)} collective-permute-done((bf16[3,64,256]{2,1,0:T(8,128)(2,1)S(1)}, bf16[3,64,256]{2,1,0:T(8,128)(2,1)S(1)}, u32[]{:S(2)}, u32[]{:S(2)}) %collective-permute-start.6) | collective-permute-done | bytes 98336 | tf_op jit(solution)/shard_map/ppermute | solution.py:12
  110.3 2.9 %all_gather.72 = bf16[3,128,512]{2,1,0:T(8,128)(2,1)S(1)} all-gather(bf16[3,128,256]{2,1,0:T(8,128)(2,1)S(1)} %fusion.34), channel_id=1, replica_groups=mesh['tm'=256,'chan'=2] {'chan'}, dimensions={2}, use_global_device_ids=true | all-gather | bytes 589824 | tf_op jit(solution)/shard_map/all_gather | solution.py:53
  118.3 11.2 %collective-permute-done.7 = bf16[3,128,256]{2,1,0:T(8,128)(2,1)S(1)} collective-permute-done((bf16[3,128,256]{2,1,0:T(8,128)(2,1)S(1)}, bf16[3,128,256]{2,1,0:T(8,128)(2,1)S(1)}, u32[]{:S(2)}, u32[]{:S(2)}) %collective-permute-start.7) | collective-permute-done | bytes 196640 | tf_op jit(solution)/shard_map/ppermute | solution.py:12
  129.6 2.9 %all_gather.74 = bf16[3,128,512]{2,1,0:T(8,128)(2,1)S(1)} all-gather(bf16[3,128,256]{2,1,0:T(8,128)(2,1)S(1)} %fusion.36), channel_id=1, replica_groups=mesh['tm'=256,'chan'=2] {'chan'}, dimensions={2}, use_global_device_ids=true | all-gather | bytes 589824 | tf_op jit(solution)/shard_map/all_gather | solution.py:53
  137.6 11.5 %collective-permute-done.8 = bf16[3,128,256]{2,1,0:T(8,128)(2,1)S(1)} collective-permute-done((bf16[3,128,256]{2,1,0:T(8,128)(2,1)S(1)}, bf16[3,128,256]{2,1,0:T(8,128)(2,1)S(1)}, u32[]{:S(2)}, u32[]{:S(2)}) %collective-permute-start.8) | collective-permute-done | bytes 196640 | tf_op jit(solution)/shard_map/ppermute | solution.py:12
  149.2 2.9 %all_gather.76 = bf16[3,128,512]{2,1,0:T(8,128)(2,1)S(1)} all-gather(bf16[3,128,256]{2,1,0:T(8,128)(2,1)S(1)} %fusion.38), channel_id=1, replica_groups=mesh['tm'=256,'chan'=2] {'chan'}, dimensions={2}, use_global_device_ids=true | all-gather | bytes 589824 | tf_op jit(solution)/shard_map/all_gather | solution.py:53
  152.7 2.1 %all-gather.8 = bf16[3,128,1,512]{3,1,2,0:T(8,128)(2,1)S(1)} all-gather(bf16[3,128,1,256]{3,1,2,0:T(8,128)(2,1)S(1)} %fusion.120), channel_id=10, replica_groups=mesh['tm'=256,'chan'=2] {'chan'}, dimensions={3}, use_global_device_ids=true | all-gather | bytes 589824 | tf_op jit(solution)/shard_map/all_gather | solution.py:60
  157.2 9.1 %collective-permute-done.9 = bf16[3,128,256]{2,1,0:T(8,128)(2,1)S(1)} collective-permute-done((bf16[3,128,256]{2,1,0:T(8,128)(2,1)S(1)}, bf16[3,128,256]{2,1,0:T(8,128)(2,1)S(1)}, u32[]{:S(2)}, u32[]{:S(2)}) %collective-permute-start.9) | collective-permute-done | bytes 196640 | tf_op jit(solution)/shard_map/ppermute | solution.py:12
  166.4 3.0 %all_gather.78 = bf16[3,128,512]{2,1,0:T(8,128)(2,1)S(1)} all-gather(bf16[3,128,256]{2,1,0:T(8,128)(2,1)S(1)} %fusion.40), channel_id=1, replica_groups=mesh['tm'=256,'chan'=2] {'chan'}, dimensions={2}, use_global_device_ids=true | all-gather | bytes 589824 | tf_op jit(solution)/shard_map/all_gather | solution.py:53
  (87 shorter events, 46.1 us)
Async XLA Ops:
  1.3 9.2 %copy-start.3 = (f32[10,2,256]{2,1,0:T(2,128)S(1)}, f32[10,2,256]{2,1,0:T(2,128)}, u32[]{:S(2)}) copy-start(f32[10,2,256]{2,1,0:T(2,128)} %param.6) | copy-start | bytes 61444
  1.3 9.9 %copy-start.2 = (bf16[3,128,256]{2,1,0:T(8,128)(2,1)S(1)}, bf16[3,128,256]{2,1,0:T(8,128)(2,1)}, u32[]{:S(2)}) copy-start(bf16[3,128,256]{2,1,0:T(8,128)(2,1)} %param.5) | copy-start | bytes 589828
  1.4 9.9 %collective-permute-start = (bf16[3,1,256]{2,1,0:T(2,128)(2,1)S(1)}, bf16[3,1,256]{2,1,0:T(2,128)(2,1)S(1)}, u32[]{:S(2)}, u32[]{:S(2)}) collective-permute-start(bf16[3,1,256]{2,1,0:T(2,128)(2,1)S(1)} %slice.253), channel_id=1, source_target_pairs={{0,2},{2,4},{4,6},{6,8},{8,10},{10,12},{12,14},{14,16},{16,18},{18... | collective-permute-start | bytes 4616 | tf_op jit(solution)/shard_map/ppermute | solution.py:12
  10.6 7.1 %copy-start.1 = (bf16[10,512,256]{2,1,0:T(8,128)(2,1)S(1)}, bf16[10,512,256]{2,1,0:T(8,128)(2,1)}, u32[]{:S(2)}) copy-start(bf16[10,512,256]{2,1,0:T(8,128)(2,1)} %param.8) | copy-start | bytes 7864324
  11.3 8.6 %copy-start = (bf16[10,512,256]{2,1,0:T(8,128)(2,1)S(1)}, bf16[10,512,256]{2,1,0:T(8,128)(2,1)}, u32[]{:S(2)}) copy-start(bf16[10,512,256]{2,1,0:T(8,128)(2,1)} %param.9) | copy-start | bytes 7864324
  18.0 9.8 %collective-permute-start.1 = (bf16[3,2,256]{2,1,0:T(2,128)(2,1)S(1)}, bf16[3,2,256]{2,1,0:T(2,128)(2,1)S(1)}, u32[]{:S(2)}, u32[]{:S(2)}) collective-permute-start(bf16[3,2,256]{2,1,0:T(2,128)(2,1)S(1)} %slice.338), channel_id=1, source_target_pairs={{0,2},{2,4},{4,6},{6,8},{8,10},{10,12},{12,14},{14,16},{16,18},{18... | collective-permute-start | bytes 9224 | tf_op jit(solution)/shard_map/ppermute | solution.py:12
  34.0 9.8 %collective-permute-start.2 = (bf16[3,4,256]{2,1,0:T(4,128)(2,1)S(1)}, bf16[3,4,256]{2,1,0:T(4,128)(2,1)S(1)}, u32[]{:S(2)}, u32[]{:S(2)}) collective-permute-start(bf16[3,4,256]{2,1,0:T(4,128)(2,1)S(1)} %slice.342), channel_id=1, source_target_pairs={{0,2},{2,4},{4,6},{6,8},{8,10},{10,12},{12,14},{14,16},{16,18},{18... | collective-permute-start | bytes 18440 | tf_op jit(solution)/shard_map/ppermute | solution.py:12
  50.0 9.9 %collective-permute-start.3 = (bf16[3,8,256]{2,1,0:T(8,128)(2,1)S(1)}, bf16[3,8,256]{2,1,0:T(8,128)(2,1)S(1)}, u32[]{:S(2)}, u32[]{:S(2)}) collective-permute-start(bf16[3,8,256]{2,1,0:T(8,128)(2,1)S(1)} %slice.346), channel_id=1, source_target_pairs={{0,2},{2,4},{4,6},{6,8},{8,10},{10,12},{12,14},{14,16},{16,18},{18... | collective-permute-start | bytes 36872 | tf_op jit(solution)/shard_map/ppermute | solution.py:12
  66.1 10.0 %collective-permute-start.4 = (bf16[3,16,256]{2,1,0:T(8,128)(2,1)S(1)}, bf16[3,16,256]{2,1,0:T(8,128)(2,1)S(1)}, u32[]{:S(2)}, u32[]{:S(2)}) collective-permute-start(bf16[3,16,256]{2,1,0:T(8,128)(2,1)S(1)} %slice.350), channel_id=1, source_target_pairs={{0,2},{2,4},{4,6},{6,8},{8,10},{10,12},{12,14},{14,16},{16,18},{18... | collective-permute-start | bytes 73736 | tf_op jit(solution)/shard_map/ppermute | solution.py:12
  82.4 10.3 %collective-permute-start.5 = (bf16[3,32,256]{2,1,0:T(8,128)(2,1)S(1)}, bf16[3,32,256]{2,1,0:T(8,128)(2,1)S(1)}, u32[]{:S(2)}, u32[]{:S(2)}) collective-permute-start(bf16[3,32,256]{2,1,0:T(8,128)(2,1)S(1)} %slice.354), channel_id=1, source_target_pairs={{0,2},{2,4},{4,6},{6,8},{8,10},{10,12},{12,14},{14,16},{16,18},{18... | collective-permute-start | bytes 147464 | tf_op jit(solution)/shard_map/ppermute | solution.py:12
  98.9 11.3 %collective-permute-start.6 = (bf16[3,64,256]{2,1,0:T(8,128)(2,1)S(1)}, bf16[3,64,256]{2,1,0:T(8,128)(2,1)S(1)}, u32[]{:S(2)}, u32[]{:S(2)}) collective-permute-start(bf16[3,64,256]{2,1,0:T(8,128)(2,1)S(1)} %get-tuple-element.12), channel_id=1, source_target_pairs={{0,2},{2,4},{4,6},{6,8},{8,10},{10,12},{12,14},{14,16},{16,18},{18... | collective-permute-start | bytes 294920 | tf_op jit(solution)/shard_map/ppermute | solution.py:12
  116.1 13.4 %collective-permute-start.7 = (bf16[3,128,256]{2,1,0:T(8,128)(2,1)S(1)}, bf16[3,128,256]{2,1,0:T(8,128)(2,1)S(1)}, u32[]{:S(2)}, u32[]{:S(2)}) collective-permute-start(bf16[3,128,256]{2,1,0:T(8,128)(2,1)S(1)} %fusion.6), channel_id=1, source_target_pairs={{0,2},{2,4},{4,6},{6,8},{8,10},{10,12},{12,14},{14,16},{16,18},{18... | collective-permute-start | bytes 589832 | tf_op jit(solution)/shard_map/ppermute | solution.py:12
  135.4 13.7 %collective-permute-start.8 = (bf16[3,128,256]{2,1,0:T(8,128)(2,1)S(1)}, bf16[3,128,256]{2,1,0:T(8,128)(2,1)S(1)}, u32[]{:S(2)}, u32[]{:S(2)}) collective-permute-start(bf16[3,128,256]{2,1,0:T(8,128)(2,1)S(1)} %fusion.7), channel_id=1, source_target_pairs={{0,4},{2,6},{4,8},{6,10},{8,12},{10,14},{12,16},{14,18},{16,20},{1... | collective-permute-start | bytes 589832 | tf_op jit(solution)/shard_map/ppermute | solution.py:12
  155.0 11.3 %collective-permute-start.9 = (bf16[3,128,256]{2,1,0:T(8,128)(2,1)S(1)}, bf16[3,128,256]{2,1,0:T(8,128)(2,1)S(1)}, u32[]{:S(2)}, u32[]{:S(2)}) collective-permute-start(bf16[3,128,256]{2,1,0:T(8,128)(2,1)S(1)} %fusion.8), channel_id=1, source_target_pairs={{0,8},{2,10},{4,12},{6,14},{8,16},{10,18},{12,20},{14,22},{16,24},... | collective-permute-start | bytes 589832 | tf_op jit(solution)/shard_map/ppermute | solution.py:12
where the time goes:
time: 175 us; the launch traced here: 174 us
  waiting for transfers between devices  80.2 us (46%)
  blocking collectives  52.5 us (30%)
  starting transfers between devices  20.5 us (12%)
  matrix products  10.2 us (6%)
  local copies, waits for them, and re-layouts  6.8 us (4%)
  other arithmetic  2.5 us (1%)
    ppermute x10, waiting for transfers between devices, shifted(): lax.ppermute(value, axis, [(source, source + steps) for source in range(l...  80.2 us
    all_gather x10, blocking collectives, local(): lax.all_gather(conv, 'chan', axis=2, tiled=True)  31.6 us
    all_gather x10, blocking collectives, local(): piece = lax.all_gather(gated, 'chan', axis=2, tiled=True)  20.9 us
    ppermute x10, starting transfers between devices, shifted(): lax.ppermute(value, axis, [(source, source + steps) for source in range(l...  20.5 us
    slice x1, local copies, waits for them, and re-layouts, local(): gate_w = w_gate[layer]  5.96 us
    dot_general x10, matrix products, local(): jnp.einsum('stc,cko->stko', lax.all_gather(conv, 'chan', axis=2, tiled=Tr...  3.61 us
  transfers between devices with their start and end apart: 10, of which 10 were waited for; matrix products, arithmetic and copies ran while one was open for 5% of the time, Pallas kernels for 0%

commit v1 on v0

v1 whole, which is shorter than its diff:
```python
import jax
import jax.numpy as jnp
from jax import lax
from jax.experimental import pallas as pl
from jax.experimental.pallas import tpu as pltpu
from jax.sharding import PartitionSpec as P


PAD = 16
A0 = PAD
A_FIRST = (0, 0, 0, 16, 32, 64, 128)
B_FIRST = (0, 0, 0, 0, 16, 32, 64)
HALVES = (slice(0, 256), slice(256, 512))
BF = jnp.bfloat16
F32 = jnp.float32


def from_earlier(value, steps):
    count = lax.axis_size("tm")
    return lax.ppermute(value, "tm", [(i, i + steps) for i in range(count - steps)])


def from_two(value, steps):
    count = lax.axis_size("tm")
    pairs = [(2 * i + c, 2 * (i + steps[c]) + c) for c in range(2) for i in range(count - steps[c])]
    return lax.ppermute(value, ("tm", "chan"), pairs)


def other_core(value):
    return lax.ppermute(value, "chan", [(0, 1), (1, 0)])


def dot(a, b):
    return jnp.dot(a, b, preferred_element_type=F32)


def columns():
    core = lax.axis_index("chan")
    own = pl.ds(pl.multiple_of(core * 256, 256), 256)
    other = pl.ds(pl.multiple_of((1 - core) * 256, 256), 256)
    return core, own, other


def rows_own_first(w, order):
    return jnp.concatenate([w[rows] for rows in order], axis=0)


def gated_units(y_ref, z_ref, rows, weights, order):
    y = y_ref[0:rows]
    for w, cols in zip(weights, HALVES):
        f = dot(y, rows_own_first(w.at[0], order))
        g = dot(y, rows_own_first(w.at[1], order))
        z_ref[0:rows, cols] = (jnp.tanh(f) * (0.5 + 0.5 * jnp.tanh(0.5 * g))).astype(BF)


def first_kernel(own, h1, h2, t_own, t_oth, g_own, g_oth, r_own, r_oth, x_out, z_out, taps, xa, xb, xp, y, z):
    core, *order = columns()
    for part, cols in zip((t_own, t_oth), HALVES):
        taps[:, :, cols] = part[...]
    zero = jnp.zeros((PAD, 512), F32)
    xa[0:PAD] = zero
    xb[:, 0:PAD] = jnp.zeros((4, PAD, 128), F32)
    xp[0:PAD] = zero
    blocks = ((h2, 1), (h1, 1), (h2, 0), (h1, 0))

    def load(rows, source):
        for given, cols in zip(order, HALVES):
            xa[rows, cols] = source[core, :, given].astype(F32)
            shared = source[2, :, given].astype(F32)
            for j in range(2):
                xb[cols.start // 128 + j, rows] = shared[:, 128 * j : 128 * j + 128]

    for k, (h, i) in enumerate(blocks):
        load(slice(A0 + 128 * k, A0 + 128 * k + 128), h.at[i])
    load(slice(A0 + 512, A0 + 640), own)

    for layer in range(7):
        delay = 2**layer
        first, first_b = A_FIRST[layer], B_FIRST[layer]
        na, nb = 640 - first, 320 - first_b
        rows = na + nb
        t0, t1 = taps[layer, 0:1], taps[layer, 1:2]
        s = A0 + first
        y[0:na] = (t0 * xa[s - delay : s - delay + na] + t1 * xa[s : s + na]).astype(BF)
        if layer == 0:
            for c in range(2):

                @pl.when(core == c)
                def _(c=c):
                    for j in range(4):
                        lanes = slice(128 * j, 128 * j + 128)
                        now = xb[j, pl.ds(PAD + c, 320, stride=2)]
                        before = xb[j, pl.ds(PAD + c - 1, 320, stride=2)]
                        y[640:960, lanes] = (t0[:, lanes] * before + t1[:, lanes] * now).astype(BF)
                        xp[PAD : PAD + 320, lanes] = now

        else:
            s = PAD + first_b
            half = delay // 2
            y[na:rows] = (t0 * xp[s - half : s - half + nb] + t1 * xp[s : s + nb]).astype(BF)
        gated_units(y, z, rows, (g_own.at[layer], g_oth.at[layer]), order)
        z_out[layer, 0:128] = z[na - 128 : na]
        z_out[layer, 128:192] = z[rows - 64 : rows]
        zv = z[0:rows]
        for w, cols in zip((r_own, r_oth), HALVES):
            u = dot(zv, rows_own_first(w.at[layer], order))
            for ref, s, n, at in ((xa, A0 + first, na, 0), (xp, PAD + first_b, nb, na)):
                ref[s : s + n, cols] = (ref[s : s + n, cols] + u[at : at + n]).astype(BF).astype(F32)

    def block(k):
        a, b = A0 + 512 - 128 * k, PAD + 256 - 64 * k
        return ((xa, slice(a, a + 128)), (xp, slice(b, b + 64)))

    for layer, targets, far in ((7, (0, 2), 1), (8, (0,), 2)):
        t0, t1 = taps[layer, 0:1], taps[layer, 1:2]
        at = 0
        for k in targets:
            for (ref, now), (_, before) in zip(block(k), block(k + far)):
                n = now.stop - now.start
                y[at : at + n] = (t0 * ref[before] + t1 * ref[now]).astype(BF)
                at += n
        rows = at
        gated_units(y, z, rows, (g_own.at[layer], g_oth.at[layer]), order)
        z_out[layer] = z[0:192]
        zv = z[0:rows]
        for w, cols in zip((r_own, r_oth), HALVES):
            u = dot(zv, rows_own_first(w.at[layer], order))
            at = 0
            for k in targets:
                for ref, now in block(k):
                    n = now.stop - now.start
                    new = (ref[now, cols] + u[at : at + n]).astype(BF)
                    if layer == 8:
                        x_out[at : at + n, cols] = new
                    else:
                        ref[now, cols] = new.astype(F32)
                    at += n


def last_layer(x0, x4, skip, taps, g_own, g_oth, r_own, r_oth, s_own, s_oth, out, y, z):
    _, *order = columns()
    t0, t1 = taps[9, 0:1], taps[9, 1:2]
    y[...] = (t0 * x4[...].astype(F32) + t1 * x0[...].astype(F32)).astype(BF)
    gated_units(y, z, 192, (g_own.at[9], g_oth.at[9]), order)
    zv = z[...]
    for r, s, cols in zip((r_own, r_oth), (s_own, s_oth), HALVES):
        out[0:192, cols] = (x0[:, cols].astype(F32) + dot(zv, rows_own_first(r.at[9], order))).astype(BF)
        out[192:384, cols] = (skip[:, cols] + dot(zv, rows_own_first(s.at[9], order))).astype(BF)


def skip_kernel(z, s_own, s_oth, out):
    _, *order = columns()
    for s, cols in zip((s_own, s_oth), HALVES):
        total = dot(z[0], rows_own_first(s.at[0], order))
        for layer in range(1, 9):
            total = total + dot(z[layer], rows_own_first(s.at[layer], order))
        out[:, cols] = total


def outputs_kernel(g, stream, skips, mixed):
    core = lax.axis_index("chan")
    for half in range(2):

        @pl.when(core == half)
        def _(half=half):
            for out, at in ((stream, 0), (skips, 192)):
                for k in range(2):
                    cols = HALVES[0 if k == half else 1]
                    out[k] = g[k, at : at + 128, cols]
                    for j in range(2):
                        lanes = slice(cols.start + 128 * j, cols.start + 128 * j + 128)
                        mixed[j, pl.ds(k, 64, stride=2)] = g[k, at + 128 : at + 192, lanes].astype(F32)
                for j in range(2):
                    out[2, :, 128 * j : 128 * j + 128] = mixed[j].astype(BF)


def call(body, inputs, outs, scratch, flops, space=pltpu.VMEM):
    moved = sum(v.size * v.dtype.itemsize for v in inputs)
    vmem = pl.BlockSpec(memory_space=pltpu.VMEM)
    return pl.pallas_call(
        body,
        out_shape=outs,
        in_specs=[pl.BlockSpec(memory_space=space)] * len(inputs),
        out_specs=jax.tree.map(lambda _: vmem, outs),
        scratch_shapes=scratch,
        cost_estimate=pl.CostEstimate(flops=flops, bytes_accessed=moved, transcendentals=0),
        compiler_params=pltpu.CompilerParams(vmem_limit_bytes=24 * 2**20),
    )(*inputs)


def relayout_kernel(w, out, raw, sems):
    copies = [pltpu.make_async_copy(w.at[layer], raw.at[layer], sems.at[layer]) for layer in range(10)]
    for copy in copies:
        copy.start()
    for layer in range(10):
        copies[layer].wait()
        both = raw[layer].reshape(512, 512)
        out[layer, 0] = both[:, :256]
        out[layer, 1] = both[:, 256:]


def local(signal, taps, w_gate, w_res, w_skip):
    sds = jax.ShapeDtypeStruct
    vm = pltpu.VMEM
    own = lax.all_gather(signal, "chan", axis=2, tiled=True)
    h1 = from_two(own, (1, 3))
    h2 = from_two(own, (2, 4))
    r_oth = other_core(w_res)
    g_own = call(
        relayout_kernel,
        [w_gate],
        sds((10, 2, 512, 256), BF),
        [vm((10, 512, 2, 256), BF), pltpu.SemaphoreType.DMA((10,))],
        10**7,
        pltpu.HBM,
    )
    g_oth = other_core(g_own)
    t_oth = other_core(taps)
    s_oth = other_core(w_skip)
    h1 = lax.all_gather(h1, "chan", axis=0)
    h2 = lax.all_gather(h2, "chan", axis=0)
    weights = [g_own, g_oth, w_res, r_oth]
    x9, zs, taps_all = call(
        first_kernel,
        [own, h1, h2, taps, t_oth, *weights],
        (sds((192, 512), BF), sds((9, 192, 512), BF), sds((10, 2, 512), F32)),
        [
            vm((PAD + 640, 512), F32),
            vm((4, PAD + 640, 128), F32),
            vm((PAD + 320, 512), F32),
            vm((960, 512), BF),
            vm((960, 512), BF),
        ],
        7000 * 512 * 1536 * 2,
    )
    x9_far = from_earlier(x9, 4)
    skip = call(skip_kernel, [zs, w_skip, s_oth], sds((192, 512), F32), [], 9 * 192 * 512 * 512 * 2)
    both = call(
        last_layer,
        [x9, x9_far, skip, taps_all, *weights, w_skip, s_oth],
        sds((384, 512), BF),
        [vm((192, 512), BF), vm((192, 512), BF)],
        192 * 512 * 2048 * 2,
    )
    both = lax.all_gather(both, "chan", axis=0)
    return call(outputs_kernel, [both], (sds((3, 128, 256), BF), sds((3, 128, 256), BF)), [vm((2, 128, 128), F32)], 1)


def solution(mesh):
    in_specs = (
        P(None, "tm", "chan"),
        P(None, None, "chan"),
        P(None, None, None, "chan"),
        P(None, None, "chan"),
        P(None, None, "chan"),
    )
    out_specs = (P(None, "tm", "chan"), P(None, "tm", "chan"))
    return jax.shard_map(local, mesh=mesh, in_specs=in_specs, out_specs=out_specs, check_vma=False)
```

time: 175 us -> 84.6 us (0.48)
  the two profiles are of different devices: /device:TPU:257 before, /device:TPU:259 now
where the time goes in v1:
time: 84.6 us; the launch traced here: 84.3 us
  blocking collectives  29.2 us (35%)
  Pallas kernels  20 us (24%)
  starting transfers between devices  17.1 us (20%)
  waiting for transfers between devices  14.6 us (17%)
  local copies, waits for them, and re-layouts  2.64 us (3%)
    pallas_call x5, Pallas kernels, call(): pl.pallas_call(body, out_shape=outs, in_specs=[pl.BlockSpec(memory_space=...  20 us
    all_gather x1, blocking collectives, local(): h2 = lax.all_gather(h2, 'chan', axis=0)  11.8 us
    all_gather x1, blocking collectives, local(): own = lax.all_gather(signal, 'chan', axis=2, tiled=True)  11.7 us
    ppermute x4, starting transfers between devices, other_core(): return lax.ppermute(value, 'chan', [(0, 1), (1, 0)])  8.82 us
    ppermute x1, waiting for transfers between devices, from_earlier(): lax.ppermute(value, 'tm', [(i, i + steps) for i in range(count - steps)])  8.26 us
    ppermute x2, starting transfers between devices, from_two(): return lax.ppermute(value, ('tm', 'chan'), pairs)  6.37 us
    ppermute x2, waiting for transfers between devices, from_two(): return lax.ppermute(value, ('tm', 'chan'), pairs)  6.35 us
    all_gather x1, blocking collectives, local(): both = lax.all_gather(both, 'chan', axis=0)  3.23 us
  transfers between devices with their start and end apart: 7, of which 2 were waited for; matrix products, arithmetic and copies ran while one was open for 0% of the time, Pallas kernels for 18%

profile of v1, /device:TPU:259, one launch (start us, length us, event | category | flops | bytes accessed | tf_op | source)
XLA Modules:
  0.0 84.3 jit_solution(16765705270909487712)
XLA Ops:
  0.7 2.6 %copy-done.1 = bf16[10,512,2,256]{3,2,1,0:T(2,128)(2,1)S(1)} copy-done((bf16[10,512,2,256]{3,2,1,0:T(2,128)(2,1)S(1)}, bf16[10,512,2,256]{3,2,1,0:T(2,128)(2,1)}, u32[]{:S(2)}) %copy-start.1) | copy-done | bytes 5242904
  3.3 3.4 %shard_map.68.g_own = bf16[10,2,512,256]{3,2,1,0:T(8,128)(2,1)S(1)} custom-call(bf16[10,512,2,256]{3,2,1,0:T(2,128)(2,1)S(1)} %copy-done.1), custom_call_target="tpu_custom_call" | custom-call | flops 10000000 | bytes 5242880 | tf_op jit(solution)/shard_map/pallas_call | solution.py:180
  6.7 2.6 %collective-permute-start.3 = (bf16[10,2,512,256]{3,2,1,0:T(8,128)(2,1)S(1)}, bf16[10,2,512,256]{3,2,1,0:T(8,128)(2,1)S(1)}, u32[]{:S(2)}, u32[]{:S(2)}) collective-permute-start(bf16[10,2,512,256]{3,2,1,0:T(8,128)(2,1)S(1)} %shard_map.68.g_own), channel_id=1, source_target_pairs={{0,1},{1,0},{2,3},{3,2},{4,5},{5,4},{6,7},{7,6},{8,9},{9,8},{10,11... | collective-permute-start | bytes 15728648 | tf_op jit(solution)/shard_map/ppermute | solution.py:30
  9.3 1.9 %collective-permute-start.4 = (bf16[10,512,256]{2,1,0:T(8,128)(2,1)S(1)}, bf16[10,512,256]{2,1,0:T(8,128)(2,1)S(1)}, u32[]{:S(2)}, u32[]{:S(2)}) collective-permute-start(bf16[10,512,256]{2,1,0:T(8,128)(2,1)S(1)} %copy-done.2), channel_id=1, source_target_pairs={{0,1},{1,0},{2,3},{3,2},{4,5},{5,4},{6,7},{7,6},{8,9},{9,8},{10,11... | collective-permute-start | bytes 7864328 | tf_op jit(solution)/shard_map/ppermute | solution.py:30
  11.2 2.4 %collective-permute-start.6 = (bf16[10,512,256]{2,1,0:T(8,128)(2,1)S(1)}, bf16[10,512,256]{2,1,0:T(8,128)(2,1)S(1)}, u32[]{:S(2)}, u32[]{:S(2)}) collective-permute-start(bf16[10,512,256]{2,1,0:T(8,128)(2,1)S(1)} %copy-done), channel_id=1, source_target_pairs={{0,1},{1,0},{2,3},{3,2},{4,5},{5,4},{6,7},{7,6},{8,9},{9,8},{10,11... | collective-permute-start | bytes 7864328 | tf_op jit(solution)/shard_map/ppermute | solution.py:30
  13.7 11.7 %all_gather.21.own = bf16[3,128,512]{2,1,0:T(8,128)(2,1)S(1)} all-gather(bf16[3,128,256]{2,1,0:T(8,128)(2,1)S(1)} %copy-done.4), channel_id=1, replica_groups=mesh['tm'=256,'chan'=2] {'chan'}, dimensions={2}, use_global_device_ids=true | all-gather | bytes 589824 | tf_op jit(solution)/shard_map/all_gather | solution.py:205
  25.3 3.2 %collective-permute-start = (bf16[3,128,512]{2,1,0:T(8,128)(2,1)S(1)}, bf16[3,128,512]{2,1,0:T(8,128)(2,1)S(1)}, u32[]{:S(2)}, u32[]{:S(2)}) collective-permute-start(bf16[3,128,512]{2,1,0:T(8,128)(2,1)S(1)} %all_gather.21.own), channel_id=1, source_target_pairs={{0,2},{2,4},{4,6},{6,8},{8,10},{10,12},{12,14},{14,16},{16,18},{18... | collective-permute-start | bytes 1179656 | tf_op jit(solution)/shard_map/ppermute | solution.py:26
  28.5 3.2 %collective-permute-start.1 = (bf16[3,128,512]{2,1,0:T(8,128)(2,1)S(1)}, bf16[3,128,512]{2,1,0:T(8,128)(2,1)S(1)}, u32[]{:S(2)}, u32[]{:S(2)}) collective-permute-start(bf16[3,128,512]{2,1,0:T(8,128)(2,1)S(1)} %all_gather.21.own), channel_id=1, source_target_pairs={{0,4},{2,6},{4,8},{6,10},{8,12},{10,14},{12,16},{14,18},{16,20},{1... | collective-permute-start | bytes 1179656 | tf_op jit(solution)/shard_map/ppermute | solution.py:26
  31.7 6.3 %collective-permute-done = bf16[3,128,512]{2,1,0:T(8,128)(2,1)S(1)} collective-permute-done((bf16[3,128,512]{2,1,0:T(8,128)(2,1)S(1)}, bf16[3,128,512]{2,1,0:T(8,128)(2,1)S(1)}, u32[]{:S(2)}, u32[]{:S(2)}) %collective-permute-start) | collective-permute-done | bytes 393248 | tf_op jit(solution)/shard_map/ppermute | solution.py:26
  38.1 1.9 %collective-permute-start.2 = (f32[10,2,256]{2,1,0:T(2,128)S(1)}, f32[10,2,256]{2,1,0:T(2,128)S(1)}, u32[]{:S(2)}, u32[]{:S(2)}) collective-permute-start(f32[10,2,256]{2,1,0:T(2,128)S(1)} %copy-done.3), channel_id=1, source_target_pairs={{0,1},{1,0},{2,3},{3,2},{4,5},{5,4},{6,7},{7,6},{8,9},{9,8},{10,11... | collective-permute-start | bytes 61448 | tf_op jit(solution)/shard_map/ppermute | solution.py:30
  40.0 2.5 %all-gather = bf16[6,128,512]{2,1,0:T(8,128)(2,1)S(1)} all-gather(bf16[3,128,512]{2,1,0:T(8,128)(2,1)S(1)} %collective-permute-done), channel_id=2, replica_groups=mesh['tm'=256,'chan'=2] {'chan'}, dimensions={0}, use_global_device_ids=true | all-gather | bytes 1179648 | tf_op jit(solution)/shard_map/all_gather | solution.py:220
  42.5 0.0 collective-permute-done.1
  42.5 11.8 %all-gather.1 = bf16[6,128,512]{2,1,0:T(8,128)(2,1)S(1)} all-gather(bf16[3,128,512]{2,1,0:T(8,128)(2,1)S(1)} %collective-permute-done.1), channel_id=3, replica_groups=mesh['tm'=256,'chan'=2] {'chan'}, dimensions={0}, use_global_device_ids=true | all-gather | bytes 1179648 | tf_op jit(solution)/shard_map/all_gather | solution.py:221
  54.3 0.0 collective-permute-done.2.t_oth
  54.3 0.0 collective-permute-done.4.r_oth
  54.3 0.0 collective-permute-done.3.g_oth
  54.3 14.0 %shard_map.69 = (bf16[192,512]{1,0:T(8,128)(2,1)S(1)}, bf16[9,192,512]{2,1,0:T(8,128)(2,1)S(1)}, f32[10,2,512]{2,1,0:T(2,128)S(1)}) custom-call(bf16[3,128,512]{2,1,0:T(8,128)(2,1)S(1)} %all_gather.21.own, bf16[2,3,128,512]{3,2,1,0:T(8,128)(2,1)S(1)} %bitcast.4, bf16[2,3,128,512]{3,2,1,0:T(8,128)(2,1)S(1)} %bitcast.5, f32[10,2,256]{2,1,0:T(2,128)S(1)} %copy-done.3, ...), custom_call_target="tpu_custom_call" | custom-call | flops 11010048000 | bytes 17735680 | tf_op jit(solution)/shard_map/pallas_call | solution.py:180
  68.3 1.9 %collective-permute-start.5 = (bf16[192,512]{1,0:T(8,128)(2,1)S(1)}, bf16[192,512]{1,0:T(8,128)(2,1)S(1)}, u32[]{:S(2)}, u32[]{:S(2)}) collective-permute-start(bf16[192,512]{1,0:T(8,128)(2,1)S(1)} %get-tuple-element.5.x0), channel_id=1, source_target_pairs={{0,8},{2,10},{4,12},{6,14},{8,16},{10,18},{12,20},{14,22},{16,24},... | collective-permute-start | bytes 589832 | tf_op jit(solution)/shard_map/ppermute | solution.py:20
  70.3 0.0 collective-permute-done.6.s_oth
  70.3 1.1 %shard_map.70.skip = f32[192,512]{1,0:T(8,128)S(1)} custom-call(bf16[9,192,512]{2,1,0:T(8,128)(2,1)S(1)} %get-tuple-element.6.z, bf16[10,512,256]{2,1,0:T(8,128)(2,1)S(1)} %copy-done, bf16[10,512,256]{2,1,0:T(8,128)(2,1)S(1)} %collective-permute-done.6.s_oth), custom_call_target="tpu_custom_call" | custom-call | flops 905969664 | bytes 7012352 | tf_op jit(solution)/shard_map/pallas_call | solution.py:180
  71.4 8.3 %collective-permute-done.5.x4 = bf16[192,512]{1,0:T(8,128)(2,1)S(1)} collective-permute-done((bf16[192,512]{1,0:T(8,128)(2,1)S(1)}, bf16[192,512]{1,0:T(8,128)(2,1)S(1)}, u32[]{:S(2)}, u32[]{:S(2)}) %collective-permute-start.5) | collective-permute-done | bytes 196640 | tf_op jit(solution)/shard_map/ppermute | solution.py:20
  79.6 0.7 shard_map.71
  80.3 3.2 %all-gather.2 = bf16[768,512]{1,0:T(8,128)(2,1)S(1)} all-gather(bf16[384,512]{1,0:T(8,128)(2,1)S(1)} %shard_map.71), channel_id=4, replica_groups=mesh['tm'=256,'chan'=2] {'chan'}, dimensions={0}, use_global_device_ids=true | all-gather | bytes 1179648 | tf_op jit(solution)/shard_map/all_gather | solution.py:245
  83.5 0.8 shard_map.72
  (9 shorter events, 0.0 us)
Async XLA Ops:
  0.6 10.6 %copy-start = (bf16[10,512,256]{2,1,0:T(8,128)(2,1)S(1)}, bf16[10,512,256]{2,1,0:T(8,128)(2,1)}, u32[]{:S(2)}) copy-start(bf16[10,512,256]{2,1,0:T(8,128)(2,1)} %s_own.3) | copy-start | bytes 7864324
  0.6 2.6 %copy-start.1 = (bf16[10,512,2,256]{3,2,1,0:T(2,128)(2,1)S(1)}, bf16[10,512,2,256]{3,2,1,0:T(2,128)(2,1)}, u32[]{:S(2)}) copy-start(bf16[10,512,2,256]{3,2,1,0:T(2,128)(2,1)} %w.1) | copy-start | bytes 15728644
  3.3 6.0 %copy-start.2 = (bf16[10,512,256]{2,1,0:T(8,128)(2,1)S(1)}, bf16[10,512,256]{2,1,0:T(8,128)(2,1)}, u32[]{:S(2)}) copy-start(bf16[10,512,256]{2,1,0:T(8,128)(2,1)} %r_own.3) | copy-start | bytes 7864324
  3.3 10.4 %copy-start.4 = (bf16[3,128,256]{2,1,0:T(8,128)(2,1)S(1)}, bf16[3,128,256]{2,1,0:T(8,128)(2,1)}, u32[]{:S(2)}) copy-start(bf16[3,128,256]{2,1,0:T(8,128)(2,1)} %param.5) | copy-start | bytes 589828
  3.3 34.8 %copy-start.3 = (f32[10,2,256]{2,1,0:T(2,128)S(1)}, f32[10,2,256]{2,1,0:T(2,128)}, u32[]{:S(2)}) copy-start(f32[10,2,256]{2,1,0:T(2,128)} %t_own.1) | copy-start | bytes 61444
  6.7 47.6 %collective-permute-start.3 = (bf16[10,2,512,256]{3,2,1,0:T(8,128)(2,1)S(1)}, bf16[10,2,512,256]{3,2,1,0:T(8,128)(2,1)S(1)}, u32[]{:S(2)}, u32[]{:S(2)}) collective-permute-start(bf16[10,2,512,256]{3,2,1,0:T(8,128)(2,1)S(1)} %shard_map.68.g_own), channel_id=1, source_target_pairs={{0,1},{1,0},{2,3},{3,2},{4,5},{5,4},{6,7},{7,6},{8,9},{9,8},{10,11... | collective-permute-start | bytes 15728648 | tf_op jit(solution)/shard_map/ppermute | solution.py:30
  9.3 45.0 %collective-permute-start.4 = (bf16[10,512,256]{2,1,0:T(8,128)(2,1)S(1)}, bf16[10,512,256]{2,1,0:T(8,128)(2,1)S(1)}, u32[]{:S(2)}, u32[]{:S(2)}) collective-permute-start(bf16[10,512,256]{2,1,0:T(8,128)(2,1)S(1)} %copy-done.2), channel_id=1, source_target_pairs={{0,1},{1,0},{2,3},{3,2},{4,5},{5,4},{6,7},{7,6},{8,9},{9,8},{10,11... | collective-permute-start | bytes 7864328 | tf_op jit(solution)/shard_map/ppermute | solution.py:30
  11.2 59.0 %collective-permute-start.6 = (bf16[10,512,256]{2,1,0:T(8,128)(2,1)S(1)}, bf16[10,512,256]{2,1,0:T(8,128)(2,1)S(1)}, u32[]{:S(2)}, u32[]{:S(2)}) collective-permute-start(bf16[10,512,256]{2,1,0:T(8,128)(2,1)S(1)} %copy-done), channel_id=1, source_target_pairs={{0,1},{1,0},{2,3},{3,2},{4,5},{5,4},{6,7},{7,6},{8,9},{9,8},{10,11... | collective-permute-start | bytes 7864328 | tf_op jit(solution)/shard_map/ppermute | solution.py:30
  25.3 12.7 %collective-permute-start = (bf16[3,128,512]{2,1,0:T(8,128)(2,1)S(1)}, bf16[3,128,512]{2,1,0:T(8,128)(2,1)S(1)}, u32[]{:S(2)}, u32[]{:S(2)}) collective-permute-start(bf16[3,128,512]{2,1,0:T(8,128)(2,1)S(1)} %all_gather.21.own), channel_id=1, source_target_pairs={{0,2},{2,4},{4,6},{6,8},{8,10},{10,12},{12,14},{14,16},{16,18},{18... | collective-permute-start | bytes 1179656 | tf_op jit(solution)/shard_map/ppermute | solution.py:26
  28.5 14.0 %collective-permute-start.1 = (bf16[3,128,512]{2,1,0:T(8,128)(2,1)S(1)}, bf16[3,128,512]{2,1,0:T(8,128)(2,1)S(1)}, u32[]{:S(2)}, u32[]{:S(2)}) collective-permute-start(bf16[3,128,512]{2,1,0:T(8,128)(2,1)S(1)} %all_gather.21.own), channel_id=1, source_target_pairs={{0,4},{2,6},{4,8},{6,10},{8,12},{10,14},{12,16},{14,18},{16,20},{1... | collective-permute-start | bytes 1179656 | tf_op jit(solution)/shard_map/ppermute | solution.py:26
  38.1 16.2 %collective-permute-start.2 = (f32[10,2,256]{2,1,0:T(2,128)S(1)}, f32[10,2,256]{2,1,0:T(2,128)S(1)}, u32[]{:S(2)}, u32[]{:S(2)}) collective-permute-start(f32[10,2,256]{2,1,0:T(2,128)S(1)} %copy-done.3), channel_id=1, source_target_pairs={{0,1},{1,0},{2,3},{3,2},{4,5},{5,4},{6,7},{7,6},{8,9},{9,8},{10,11... | collective-permute-start | bytes 61448 | tf_op jit(solution)/shard_map/ppermute | solution.py:30
  68.3 11.3 %collective-permute-start.5 = (bf16[192,512]{1,0:T(8,128)(2,1)S(1)}, bf16[192,512]{1,0:T(8,128)(2,1)S(1)}, u32[]{:S(2)}, u32[]{:S(2)}) collective-permute-start(bf16[192,512]{1,0:T(8,128)(2,1)S(1)} %get-tuple-element.5.x0), channel_id=1, source_target_pairs={{0,8},{2,10},{4,12},{6,14},{8,16},{10,18},{12,20},{14,22},{16,24},... | collective-permute-start | bytes 589832 | tf_op jit(solution)/shard_map/ppermute | solution.py:20

commit v2 on v1

--- a/solution.py
+++ b/solution.py
@@ -1,3 +1,5 @@
+import functools
+
 import jax
 import jax.numpy as jnp
 from jax import lax
@@ -7,6 +9,8 @@
 
 
 PAD = 16
+MIB_A, MIB_B = 47, 24
+SPLIT = 6
 A0 = PAD
 A_FIRST = (0, 0, 0, 16, 32, 64, 128)
 B_FIRST = (0, 0, 0, 0, 16, 32, 64)
@@ -34,37 +38,43 @@
     return jnp.dot(a, b, preferred_element_type=F32)
 
 
-def columns():
+def row_order():
     core = lax.axis_index("chan")
-    own = pl.ds(pl.multiple_of(core * 256, 256), 256)
-    other = pl.ds(pl.multiple_of((1 - core) * 256, 256), 256)
-    return core, own, other
-
-
-def rows_own_first(w, order):
-    return jnp.concatenate([w[rows] for rows in order], axis=0)
-
-
-def gated_units(y_ref, z_ref, rows, weights, order):
+    return core, (pl.multiple_of(core * 256, 256), pl.multiple_of(256 - core * 256, 256))
+
+
+def rows_own_first(w, order, at=0):
+    return jnp.concatenate([w[pl.ds(at + start, 256)] for start in order], axis=0)
+
+
+def gated_units(y_ref, z_ref, rows, weights, at, order):
     y = y_ref[0:rows]
     for w, cols in zip(weights, HALVES):
-        f = dot(y, rows_own_first(w.at[0], order))
-        g = dot(y, rows_own_first(w.at[1], order))
+        f = dot(y, rows_own_first(w, order, at))
+        g = dot(y, rows_own_first(w, order, at + 512))
         z_ref[0:rows, cols] = (jnp.tanh(f) * (0.5 + 0.5 * jnp.tanh(0.5 * g))).astype(BF)
 
 
-def first_kernel(own, h1, h2, t_own, t_oth, g_own, g_oth, r_own, r_oth, x_out, z_out, taps, xa, xb, xp, y, z):
-    core, *order = columns()
-    for part, cols in zip((t_own, t_oth), HALVES):
-        taps[:, :, cols] = part[...]
+def first_kernel(own, h1, h2, t_own, ga_own, ga_oth, gb_own, gb_oth, r_own, r_oth, x_out, z_out, taps, xa, xb, xp, y, z):
+    core, order = row_order()
+    taps[:, :, HALVES[0]] = t_own[...]
+    for tap in range(2):
+        at = 1024 * (10 - SPLIT) + 48 * tap
+        parts = [gb_oth[at + 16 * part : at + 16 * part + 10].astype(F32) for part in range(3)]
+        taps[:, tap, HALVES[1]] = parts[0] + parts[1] + parts[2]
+
+    def gate(layer):
+        return ((ga_own, ga_oth), 1024 * layer) if layer < SPLIT else ((gb_own, gb_oth), 1024 * (layer - SPLIT))
+
     zero = jnp.zeros((PAD, 512), F32)
     xa[0:PAD] = zero
     xb[:, 0:PAD] = jnp.zeros((4, PAD, 128), F32)
     xp[0:PAD] = zero
-    blocks = ((h2, 1), (h1, 1), (h2, 0), (h1, 0))
+    blocks = ((h2, 1), (h2, 0), (h1, 1), (h1, 0))
 
     def load(rows, source):
-        for given, cols in zip(order, HALVES):
+        for start, cols in zip(order, HALVES):
+            given = pl.ds(start, 256)
             xa[rows, cols] = source[core, :, given].astype(F32)
             shared = source[2, :, given].astype(F32)
             for j in range(2):
@@ -98,7 +108,7 @@
             s = PAD + first_b
             half = delay // 2
             y[na:rows] = (t0 * xp[s - half : s - half + nb] + t1 * xp[s : s + nb]).astype(BF)
-        gated_units(y, z, rows, (g_own.at[layer], g_oth.at[layer]), order)
+        gated_units(y, z, rows, *gate(layer), order)
         z_out[layer, 0:128] = z[na - 128 : na]
         z_out[layer, 128:192] = z[rows - 64 : rows]
         zv = z[0:rows]
@@ -120,7 +130,7 @@
                 y[at : at + n] = (t0 * ref[before] + t1 * ref[now]).astype(BF)
                 at += n
         rows = at
-        gated_units(y, z, rows, (g_own.at[layer], g_oth.at[layer]), order)
+        gated_units(y, z, rows, *gate(layer), order)
         z_out[layer] = z[0:192]
         zv = z[0:rows]
         for w, cols in zip((r_own, r_oth), HALVES):
@@ -138,10 +148,10 @@
 
 
 def last_layer(x0, x4, skip, taps, g_own, g_oth, r_own, r_oth, s_own, s_oth, out, y, z):
-    _, *order = columns()
+    _, order = row_order()
     t0, t1 = taps[9, 0:1], taps[9, 1:2]
     y[...] = (t0 * x4[...].astype(F32) + t1 * x0[...].astype(F32)).astype(BF)
-    gated_units(y, z, 192, (g_own.at[9], g_oth.at[9]), order)
+    gated_units(y, z, 192, (g_own, g_oth), 1024 * (9 - SPLIT), order)
     zv = z[...]
     for r, s, cols in zip((r_own, r_oth), (s_own, s_oth), HALVES):
         out[0:192, cols] = (x0[:, cols].astype(F32) + dot(zv, rows_own_first(r.at[9], order))).astype(BF)
@@ -149,7 +159,7 @@
 
 
 def skip_kernel(z, s_own, s_oth, out):
-    _, *order = columns()
+    _, order = row_order()
     for s, cols in zip((s_own, s_oth), HALVES):
         total = dot(z[0], rows_own_first(s.at[0], order))
         for layer in range(1, 9):
@@ -174,55 +184,69 @@
                     out[2, :, 128 * j : 128 * j + 128] = mixed[j].astype(BF)
 
 
-def call(body, inputs, outs, scratch, flops, space=pltpu.VMEM):
+def call(body, inputs, outs, scratch, flops, spaces=None, vmem_mib=24):
     moved = sum(v.size * v.dtype.itemsize for v in inputs)
     vmem = pl.BlockSpec(memory_space=pltpu.VMEM)
     return pl.pallas_call(
         body,
         out_shape=outs,
-        in_specs=[pl.BlockSpec(memory_space=space)] * len(inputs),
+        in_specs=[pl.BlockSpec(memory_space=one) for one in spaces or [pltpu.VMEM] * len(inputs)],
         out_specs=jax.tree.map(lambda _: vmem, outs),
         scratch_shapes=scratch,
         cost_estimate=pl.CostEstimate(flops=flops, bytes_accessed=moved, transcendentals=0),
-        compiler_params=pltpu.CompilerParams(vmem_limit_bytes=24 * 2**20),
+        compiler_params=pltpu.CompilerParams(vmem_limit_bytes=vmem_mib * 2**20),
     )(*inputs)
 
 
-def relayout_kernel(w, out, raw, sems):
-    copies = [pltpu.make_async_copy(w.at[layer], raw.at[layer], sems.at[layer]) for layer in range(10)]
+def relayout_kernel(first, count, *refs):
+    *taps, w, out, raw, sems = refs
+    copies = [pltpu.make_async_copy(w.at[first + i], raw.at[i], sems.at[i]) for i in range(count)]
     for copy in copies:
         copy.start()
-    for layer in range(10):
-        copies[layer].wait()
-        both = raw[layer].reshape(512, 512)
-        out[layer, 0] = both[:, :256]
-        out[layer, 1] = both[:, 256:]
+    for tap in range(2 if taps else 0):
+        rest = taps[0][:, tap]
+        for part in range(3):
+            value = rest.astype(BF)
+            rest = rest - value.astype(F32)
+            at = count * 1024 + 48 * tap + 16 * part
+            out[at : at + 10] = value
+            out[at + 10 : at + 16] = jnp.zeros((6, 256), BF)
+    for i, copy in enumerate(copies):
+        copy.wait()
+        both = raw[i].reshape(512, 512)
+        out[1024 * i : 1024 * i + 512] = both[:, :256]
+        out[1024 * i + 512 : 1024 * i + 1024] = both[:, 256:]
+
+
+def relayout(first, count, vmem_mib, w_gate, *taps):
+    return call(
+        functools.partial(relayout_kernel, first, count),
+        [*taps, w_gate],
+        jax.ShapeDtypeStruct((count * 1024 + 96 * len(taps), 256), BF),
+        [pltpu.VMEM((count, 512, 2, 256), BF), pltpu.SemaphoreType.DMA((count,))],
+        10**6,
+        [pltpu.VMEM] * len(taps) + [pltpu.HBM],
+        vmem_mib,
+    )
 
 
 def local(signal, taps, w_gate, w_res, w_skip):
     sds = jax.ShapeDtypeStruct
     vm = pltpu.VMEM
     own = lax.all_gather(signal, "chan", axis=2, tiled=True)
-    h1 = from_two(own, (1, 3))
-    h2 = from_two(own, (2, 4))
+    h1 = from_two(own, (1, 2))
+    h2 = from_two(own, (3, 4))
     r_oth = other_core(w_res)
-    g_own = call(
-        relayout_kernel,
-        [w_gate],
-        sds((10, 2, 512, 256), BF),
-        [vm((10, 512, 2, 256), BF), pltpu.SemaphoreType.DMA((10,))],
-        10**7,
-        pltpu.HBM,
-    )
-    g_oth = other_core(g_own)
-    t_oth = other_core(taps)
+    ga_own = relayout(0, SPLIT, MIB_A, w_gate)
+    ga_oth = other_core(ga_own)
+    gb_own = relayout(SPLIT, 10 - SPLIT, MIB_B, w_gate, taps)
+    gb_oth = other_core(gb_own)
     s_oth = other_core(w_skip)
     h1 = lax.all_gather(h1, "chan", axis=0)
     h2 = lax.all_gather(h2, "chan", axis=0)
-    weights = [g_own, g_oth, w_res, r_oth]
     x9, zs, taps_all = call(
         first_kernel,
-        [own, h1, h2, taps, t_oth, *weights],
+        [own, h1, h2, taps, ga_own, ga_oth, gb_own, gb_oth, w_res, r_oth],
         (sds((192, 512), BF), sds((9, 192, 512), BF), sds((10, 2, 512), F32)),
         [
             vm((PAD + 640, 512), F32),
@@ -237,7 +261,7 @@
     skip = call(skip_kernel, [zs, w_skip, s_oth], sds((192, 512), F32), [], 9 * 192 * 512 * 512 * 2)
     both = call(
         last_layer,
-        [x9, x9_far, skip, taps_all, *weights, w_skip, s_oth],
+        [x9, x9_far, skip, taps_all, gb_own, gb_oth, w_res, r_oth, w_skip, s_oth],
         sds((384, 512), BF),
         [vm((192, 512), BF), vm((192, 512), BF)],
         192 * 512 * 2048 * 2,

time: 84.6 us -> 90.8 us (1.073)
  the two profiles are of different devices: /device:TPU:259 before, /device:TPU:257 now
where the time goes in v2:
time: 90.8 us; the launch traced here: 90.5 us
  blocking collectives  26 us (29%)
  waiting for transfers between devices  25.3 us (28%)
  Pallas kernels  20.9 us (23%)
  starting transfers between devices  17.6 us (19%)
    pallas_call x6, Pallas kernels, call(): pl.pallas_call(body, out_shape=outs, in_specs=[pl.BlockSpec(memory_space=...  20.9 us
    ppermute x2, waiting for transfers between devices, from_two(): return lax.ppermute(value, ('tm', 'chan'), pairs)  17 us
    all_gather x1, blocking collectives, local(): h2 = lax.all_gather(h2, 'chan', axis=0)  9.51 us
    ppermute x4, starting transfers between devices, other_core(): return lax.ppermute(value, 'chan', [(0, 1), (1, 0)])  9.09 us
    all_gather x1, blocking collectives, local(): own = lax.all_gather(signal, 'chan', axis=2, tiled=True)  8.31 us
    ppermute x1, waiting for transfers between devices, from_earlier(): lax.ppermute(value, 'tm', [(i, i + steps) for i in range(count - steps)])  8.26 us
    ppermute x2, starting transfers between devices, from_two(): return lax.ppermute(value, ('tm', 'chan'), pairs)  6.55 us
    all_gather x1, blocking collectives, local(): h1 = lax.all_gather(h1, 'chan', axis=0)  4.92 us
  transfers between devices with their start and end apart: 7, of which 3 were waited for; matrix products, arithmetic and copies ran while one was open for 0% of the time, Pallas kernels for 18%

profile of v2, /device:TPU:257, one launch (start us, length us, event | category | flops | bytes accessed | tf_op | source)
XLA Modules:
  0.0 90.5 jit_solution(4136568832731596331)
XLA Ops:
  0.7 3.0 %shard_map.68.ga_own = bf16[6144,256]{1,0:T(8,128)(2,1)S(1)} custom-call(bf16[10,512,2,256]{3,2,1,0:T(2,128)(2,1)} %refs_1_.1), custom_call_target="tpu_custom_call" | custom-call | flops 1000000 | bytes 5242880 | tf_op jit(solution)/shard_map/pallas_call | solution.py:190
  3.7 0.0 copy-start.1
  3.7 0.0 copy-start.4
  3.7 2.8 %collective-permute-start.2 = (bf16[6144,256]{1,0:T(8,128)(2,1)S(1)}, bf16[6144,256]{1,0:T(8,128)(2,1)S(1)}, u32[]{:S(2)}, u32[]{:S(2)}) collective-permute-start(bf16[6144,256]{1,0:T(8,128)(2,1)S(1)} %shard_map.68.ga_own), channel_id=1, source_target_pairs={{0,1},{1,0},{2,3},{3,2},{4,5},{5,4},{6,7},{7,6},{8,9},{9,8},{10,11... | collective-permute-start | bytes 9437192 | tf_op jit(solution)/shard_map/ppermute | solution.py:34
  6.6 1.9 %collective-permute-start.4 = (bf16[10,512,256]{2,1,0:T(8,128)(2,1)S(1)}, bf16[10,512,256]{2,1,0:T(8,128)(2,1)S(1)}, u32[]{:S(2)}, u32[]{:S(2)}) collective-permute-start(bf16[10,512,256]{2,1,0:T(8,128)(2,1)S(1)} %copy-done.2), channel_id=1, source_target_pairs={{0,1},{1,0},{2,3},{3,2},{4,5},{5,4},{6,7},{7,6},{8,9},{9,8},{10,11... | collective-permute-start | bytes 7864328 | tf_op jit(solution)/shard_map/ppermute | solution.py:34
  8.5 1.5 %shard_map.69.gb_own.g_own = bf16[4192,256]{1,0:T(8,128)(2,1)S(1)} custom-call(f32[10,2,256]{2,1,0:T(2,128)S(1)} %copy-done.3, bf16[10,512,2,256]{3,2,1,0:T(2,128)(2,1)S(1)} %copy-done), custom_call_target="tpu_custom_call" | custom-call | flops 1000000 | bytes 5263360 | tf_op jit(solution)/shard_map/pallas_call | solution.py:190
  10.0 2.4 %collective-permute-start.3 = (bf16[4192,256]{1,0:T(8,128)(2,1)S(1)}, bf16[4192,256]{1,0:T(8,128)(2,1)S(1)}, u32[]{:S(2)}, u32[]{:S(2)}) collective-permute-start(bf16[4192,256]{1,0:T(8,128)(2,1)S(1)} %shard_map.69.gb_own.g_own), channel_id=1, source_target_pairs={{0,1},{1,0},{2,3},{3,2},{4,5},{5,4},{6,7},{7,6},{8,9},{9,8},{10,11... | collective-permute-start | bytes 6438920 | tf_op jit(solution)/shard_map/ppermute | solution.py:34
  12.4 1.9 %collective-permute-start.6 = (bf16[10,512,256]{2,1,0:T(8,128)(2,1)S(1)}, bf16[10,512,256]{2,1,0:T(8,128)(2,1)S(1)}, u32[]{:S(2)}, u32[]{:S(2)}) collective-permute-start(bf16[10,512,256]{2,1,0:T(8,128)(2,1)S(1)} %copy-done.1), channel_id=1, source_target_pairs={{0,1},{1,0},{2,3},{3,2},{4,5},{5,4},{6,7},{7,6},{8,9},{9,8},{10,11... | collective-permute-start | bytes 7864328 | tf_op jit(solution)/shard_map/ppermute | solution.py:34
  14.4 8.3 %all_gather.21.own = bf16[3,128,512]{2,1,0:T(8,128)(2,1)S(1)} all-gather(bf16[3,128,256]{2,1,0:T(8,128)(2,1)S(1)} %copy-done.4), channel_id=1, replica_groups=mesh['tm'=256,'chan'=2] {'chan'}, dimensions={2}, use_global_device_ids=true | all-gather | bytes 589824 | tf_op jit(solution)/shard_map/all_gather | solution.py:236
  22.7 4.6 %collective-permute-start = (bf16[3,128,512]{2,1,0:T(8,128)(2,1)S(1)}, bf16[3,128,512]{2,1,0:T(8,128)(2,1)S(1)}, u32[]{:S(2)}, u32[]{:S(2)}) collective-permute-start(bf16[3,128,512]{2,1,0:T(8,128)(2,1)S(1)} %all_gather.21.own), channel_id=1, source_target_pairs={{0,2},{2,4},{4,6},{6,8},{8,10},{10,12},{12,14},{14,16},{16,18},{18... | collective-permute-start | bytes 1179656 | tf_op jit(solution)/shard_map/ppermute | solution.py:30
  27.3 12.0 %collective-permute-done = bf16[3,128,512]{2,1,0:T(8,128)(2,1)S(1)} collective-permute-done((bf16[3,128,512]{2,1,0:T(8,128)(2,1)S(1)}, bf16[3,128,512]{2,1,0:T(8,128)(2,1)S(1)}, u32[]{:S(2)}, u32[]{:S(2)}) %collective-permute-start) | collective-permute-done | bytes 393248 | tf_op jit(solution)/shard_map/ppermute | solution.py:30
  39.3 1.9 %collective-permute-start.1 = (bf16[3,128,512]{2,1,0:T(8,128)(2,1)S(1)}, bf16[3,128,512]{2,1,0:T(8,128)(2,1)S(1)}, u32[]{:S(2)}, u32[]{:S(2)}) collective-permute-start(bf16[3,128,512]{2,1,0:T(8,128)(2,1)S(1)} %all_gather.21.own), channel_id=1, source_target_pairs={{0,6},{2,8},{4,10},{6,12},{8,14},{10,16},{12,18},{14,20},{16,22},{... | collective-permute-start | bytes 1179656 | tf_op jit(solution)/shard_map/ppermute | solution.py:30
  41.3 4.9 %all-gather = bf16[6,128,512]{2,1,0:T(8,128)(2,1)S(1)} all-gather(bf16[3,128,512]{2,1,0:T(8,128)(2,1)S(1)} %collective-permute-done), channel_id=2, replica_groups=mesh['tm'=256,'chan'=2] {'chan'}, dimensions={0}, use_global_device_ids=true | all-gather | bytes 1179648 | tf_op jit(solution)/shard_map/all_gather | solution.py:245
  46.2 5.0 %collective-permute-done.1 = bf16[3,128,512]{2,1,0:T(8,128)(2,1)S(1)} collective-permute-done((bf16[3,128,512]{2,1,0:T(8,128)(2,1)S(1)}, bf16[3,128,512]{2,1,0:T(8,128)(2,1)S(1)}, u32[]{:S(2)}, u32[]{:S(2)}) %collective-permute-start.1) | collective-permute-done | bytes 393248 | tf_op jit(solution)/shard_map/ppermute | solution.py:30
  51.2 9.5 %all-gather.1 = bf16[6,128,512]{2,1,0:T(8,128)(2,1)S(1)} all-gather(bf16[3,128,512]{2,1,0:T(8,128)(2,1)S(1)} %collective-permute-done.1), channel_id=3, replica_groups=mesh['tm'=256,'chan'=2] {'chan'}, dimensions={0}, use_global_device_ids=true | all-gather | bytes 1179648 | tf_op jit(solution)/shard_map/all_gather | solution.py:246
  60.7 0.0 collective-permute-done.3.gb_oth.g_oth
  60.7 13.8 %shard_map.70 = (bf16[192,512]{1,0:T(8,128)(2,1)S(1)}, bf16[9,192,512]{2,1,0:T(8,128)(2,1)S(1)}, f32[10,2,512]{2,1,0:T(2,128)S(1)}) custom-call(bf16[3,128,512]{2,1,0:T(8,128)(2,1)S(1)} %all_gather.21.own, bf16[2,3,128,512]{3,2,1,0:T(8,128)(2,1)S(1)} %bitcast.4, bf16[2,3,128,512]{3,2,1,0:T(8,128)(2,1)S(1)} %bitcast.5, f32[10,2,256]{2,1,0:T(2,128)S(1)} %copy-done.3, ...), custom_call_target="tpu_custom_call" | custom-call | flops 11010048000 | bytes 17813504 | tf_op jit(solution)/shard_map/pallas_call | solution.py:190
  74.5 1.9 %collective-permute-start.5 = (bf16[192,512]{1,0:T(8,128)(2,1)S(1)}, bf16[192,512]{1,0:T(8,128)(2,1)S(1)}, u32[]{:S(2)}, u32[]{:S(2)}) collective-permute-start(bf16[192,512]{1,0:T(8,128)(2,1)S(1)} %get-tuple-element.5.x0), channel_id=1, source_target_pairs={{0,8},{2,10},{4,12},{6,14},{8,16},{10,18},{12,20},{14,22},{16,24},... | collective-permute-start | bytes 589832 | tf_op jit(solution)/shard_map/ppermute | solution.py:24
  76.5 0.0 collective-permute-done.6.s_oth
  76.5 1.1 %shard_map.71.skip = f32[192,512]{1,0:T(8,128)S(1)} custom-call(bf16[9,192,512]{2,1,0:T(8,128)(2,1)S(1)} %get-tuple-element.6.z, bf16[10,512,256]{2,1,0:T(8,128)(2,1)S(1)} %copy-done.1, bf16[10,512,256]{2,1,0:T(8,128)(2,1)S(1)} %collective-permute-done.6.s_oth), custom_call_target="tpu_custom_call" | custom-call | flops 905969664 | bytes 7012352 | tf_op jit(solution)/shard_map/pallas_call | solution.py:190
  77.6 8.3 %collective-permute-done.5.x4 = bf16[192,512]{1,0:T(8,128)(2,1)S(1)} collective-permute-done((bf16[192,512]{1,0:T(8,128)(2,1)S(1)}, bf16[192,512]{1,0:T(8,128)(2,1)S(1)}, u32[]{:S(2)}, u32[]{:S(2)}) %collective-permute-start.5) | collective-permute-done | bytes 196640 | tf_op jit(solution)/shard_map/ppermute | solution.py:24
  85.8 0.6 shard_map.72
  86.5 3.2 %all-gather.2 = bf16[768,512]{1,0:T(8,128)(2,1)S(1)} all-gather(bf16[384,512]{1,0:T(8,128)(2,1)S(1)} %shard_map.72), channel_id=4, replica_groups=mesh['tm'=256,'chan'=2] {'chan'}, dimensions={0}, use_global_device_ids=true | all-gather | bytes 1179648 | tf_op jit(solution)/shard_map/all_gather | solution.py:269
  89.7 0.8 shard_map.73
  (10 shorter events, 0.0 us)
Async XLA Ops:
  0.6 7.9 %copy-start = (bf16[10,512,2,256]{3,2,1,0:T(2,128)(2,1)S(1)}, bf16[10,512,2,256]{3,2,1,0:T(2,128)(2,1)}, u32[]{:S(2)}) copy-start(bf16[10,512,2,256]{3,2,1,0:T(2,128)(2,1)} %refs_1_.1) | copy-start | bytes 15728644
  0.6 5.9 %copy-start.2 = (bf16[10,512,256]{2,1,0:T(8,128)(2,1)S(1)}, bf16[10,512,256]{2,1,0:T(8,128)(2,1)}, u32[]{:S(2)}) copy-start(bf16[10,512,256]{2,1,0:T(8,128)(2,1)} %r_own.3) | copy-start | bytes 7864324
  0.7 7.9 %copy-start.3 = (f32[10,2,256]{2,1,0:T(2,128)S(1)}, f32[10,2,256]{2,1,0:T(2,128)}, u32[]{:S(2)}) copy-start(f32[10,2,256]{2,1,0:T(2,128)} %t_own.1) | copy-start | bytes 61444
  3.7 8.7 %copy-start.1 = (bf16[10,512,256]{2,1,0:T(8,128)(2,1)S(1)}, bf16[10,512,256]{2,1,0:T(8,128)(2,1)}, u32[]{:S(2)}) copy-start(bf16[10,512,256]{2,1,0:T(8,128)(2,1)} %s_own.3) | copy-start | bytes 7864324
  3.7 10.7 %copy-start.4 = (bf16[3,128,256]{2,1,0:T(8,128)(2,1)S(1)}, bf16[3,128,256]{2,1,0:T(8,128)(2,1)}, u32[]{:S(2)}) copy-start(bf16[3,128,256]{2,1,0:T(8,128)(2,1)} %param.5) | copy-start | bytes 589828
  3.7 57.0 %collective-permute-start.2 = (bf16[6144,256]{1,0:T(8,128)(2,1)S(1)}, bf16[6144,256]{1,0:T(8,128)(2,1)S(1)}, u32[]{:S(2)}, u32[]{:S(2)}) collective-permute-start(bf16[6144,256]{1,0:T(8,128)(2,1)S(1)} %shard_map.68.ga_own), channel_id=1, source_target_pairs={{0,1},{1,0},{2,3},{3,2},{4,5},{5,4},{6,7},{7,6},{8,9},{9,8},{10,11... | collective-permute-start | bytes 9437192 | tf_op jit(solution)/shard_map/ppermute | solution.py:34
  6.6 54.1 %collective-permute-start.4 = (bf16[10,512,256]{2,1,0:T(8,128)(2,1)S(1)}, bf16[10,512,256]{2,1,0:T(8,128)(2,1)S(1)}, u32[]{:S(2)}, u32[]{:S(2)}) collective-permute-start(bf16[10,512,256]{2,1,0:T(8,128)(2,1)S(1)} %copy-done.2), channel_id=1, source_target_pairs={{0,1},{1,0},{2,3},{3,2},{4,5},{5,4},{6,7},{7,6},{8,9},{9,8},{10,11... | collective-permute-start | bytes 7864328 | tf_op jit(solution)/shard_map/ppermute | solution.py:34
  10.0 50.7 %collective-permute-start.3 = (bf16[4192,256]{1,0:T(8,128)(2,1)S(1)}, bf16[4192,256]{1,0:T(8,128)(2,1)S(1)}, u32[]{:S(2)}, u32[]{:S(2)}) collective-permute-start(bf16[4192,256]{1,0:T(8,128)(2,1)S(1)} %shard_map.69.gb_own.g_own), channel_id=1, source_target_pairs={{0,1},{1,0},{2,3},{3,2},{4,5},{5,4},{6,7},{7,6},{8,9},{9,8},{10,11... | collective-permute-start | bytes 6438920 | tf_op jit(solution)/shard_map/ppermute | solution.py:34
  12.4 64.0 %collective-permute-start.6 = (bf16[10,512,256]{2,1,0:T(8,128)(2,1)S(1)}, bf16[10,512,256]{2,1,0:T(8,128)(2,1)S(1)}, u32[]{:S(2)}, u32[]{:S(2)}) collective-permute-start(bf16[10,512,256]{2,1,0:T(8,128)(2,1)S(1)} %copy-done.1), channel_id=1, source_target_pairs={{0,1},{1,0},{2,3},{3,2},{4,5},{5,4},{6,7},{7,6},{8,9},{9,8},{10,11... | collective-permute-start | bytes 7864328 | tf_op jit(solution)/shard_map/ppermute | solution.py:34
  22.7 16.6 %collective-permute-start = (bf16[3,128,512]{2,1,0:T(8,128)(2,1)S(1)}, bf16[3,128,512]{2,1,0:T(8,128)(2,1)S(1)}, u32[]{:S(2)}, u32[]{:S(2)}) collective-permute-start(bf16[3,128,512]{2,1,0:T(8,128)(2,1)S(1)} %all_gather.21.own), channel_id=1, source_target_pairs={{0,2},{2,4},{4,6},{6,8},{8,10},{10,12},{12,14},{14,16},{16,18},{18... | collective-permute-start | bytes 1179656 | tf_op jit(solution)/shard_map/ppermute | solution.py:30
  39.3 11.8 %collective-permute-start.1 = (bf16[3,128,512]{2,1,0:T(8,128)(2,1)S(1)}, bf16[3,128,512]{2,1,0:T(8,128)(2,1)S(1)}, u32[]{:S(2)}, u32[]{:S(2)}) collective-permute-start(bf16[3,128,512]{2,1,0:T(8,128)(2,1)S(1)} %all_gather.21.own), channel_id=1, source_target_pairs={{0,6},{2,8},{4,10},{6,12},{8,14},{10,16},{12,18},{14,20},{16,22},{... | collective-permute-start | bytes 1179656 | tf_op jit(solution)/shard_map/ppermute | solution.py:30
  74.5 11.3 %collective-permute-start.5 = (bf16[192,512]{1,0:T(8,128)(2,1)S(1)}, bf16[192,512]{1,0:T(8,128)(2,1)S(1)}, u32[]{:S(2)}, u32[]{:S(2)}) collective-permute-start(bf16[192,512]{1,0:T(8,128)(2,1)S(1)} %get-tuple-element.5.x0), channel_id=1, source_target_pairs={{0,8},{2,10},{4,12},{6,14},{8,16},{10,18},{12,20},{14,22},{16,24},... | collective-permute-start | bytes 589832 | tf_op jit(solution)/shard_map/ppermute | solution.py:24

commit v3 on v2

--- a/solution.py
+++ b/solution.py
@@ -10,7 +10,7 @@
 
 PAD = 16
 MIB_A, MIB_B = 47, 24
-SPLIT = 6
+SPLIT = 5
 A0 = PAD
 A_FIRST = (0, 0, 0, 16, 32, 64, 128)
 B_FIRST = (0, 0, 0, 0, 16, 32, 64)
@@ -70,7 +70,7 @@
     xa[0:PAD] = zero
     xb[:, 0:PAD] = jnp.zeros((4, PAD, 128), F32)
     xp[0:PAD] = zero
-    blocks = ((h2, 1), (h2, 0), (h1, 1), (h1, 0))
+    blocks = ((h2, 0), (h2, 1), (h1, 1), (h1, 0))
 
     def load(rows, source):
         for start, cols in zip(order, HALVES):
@@ -93,29 +93,25 @@
         s = A0 + first
         y[0:na] = (t0 * xa[s - delay : s - delay + na] + t1 * xa[s : s + na]).astype(BF)
         if layer == 0:
-            for c in range(2):
-
-                @pl.when(core == c)
-                def _(c=c):
-                    for j in range(4):
-                        lanes = slice(128 * j, 128 * j + 128)
-                        now = xb[j, pl.ds(PAD + c, 320, stride=2)]
-                        before = xb[j, pl.ds(PAD + c - 1, 320, stride=2)]
-                        y[640:960, lanes] = (t0[:, lanes] * before + t1[:, lanes] * now).astype(BF)
-                        xp[PAD : PAD + 320, lanes] = now
-
+            for j in range(4):
+                lanes = slice(128 * j, 128 * j + 128)
+                now = xb[j, pl.ds(PAD + core, 320, stride=2)]
+                before = xb[j, pl.ds(PAD - 1 + core, 320, stride=2)]
+                y[640:960, lanes] = (t0[:, lanes] * before + t1[:, lanes] * now).astype(BF)
+                xp[PAD : PAD + 320, lanes] = now
         else:
             s = PAD + first_b
             half = delay // 2
             y[na:rows] = (t0 * xp[s - half : s - half + nb] + t1 * xp[s : s + nb]).astype(BF)
-        gated_units(y, z, rows, *gate(layer), order)
+        for lo, hi in ((0, na), (na, rows)):
+            gated_units(y.at[lo:hi], z.at[lo:hi], hi - lo, *gate(layer), order)
         z_out[layer, 0:128] = z[na - 128 : na]
         z_out[layer, 128:192] = z[rows - 64 : rows]
-        zv = z[0:rows]
-        for w, cols in zip((r_own, r_oth), HALVES):
-            u = dot(zv, rows_own_first(w.at[layer], order))
-            for ref, s, n, at in ((xa, A0 + first, na, 0), (xp, PAD + first_b, nb, na)):
-                ref[s : s + n, cols] = (ref[s : s + n, cols] + u[at : at + n]).astype(BF).astype(F32)
+        for ref, s, n, at in ((xa, A0 + first, na, 0), (xp, PAD + first_b, nb, na)):
+            zv = z[at : at + n]
+            for w, cols in zip((r_own, r_oth), HALVES):
+                u = dot(zv, rows_own_first(w.at[layer], order))
+                ref[s : s + n, cols] = (ref[s : s + n, cols] + u).astype(BF).astype(F32)
 
     def block(k):
         a, b = A0 + 512 - 128 * k, PAD + 256 - 64 * k
@@ -147,41 +143,45 @@
                     at += n
 
 
-def last_layer(x0, x4, skip, taps, g_own, g_oth, r_own, r_oth, s_own, s_oth, out, y, z):
+def last_layer(x0, x4, taps, g_own, g_oth, r_own, r_oth, out, y):
     _, order = row_order()
     t0, t1 = taps[9, 0:1], taps[9, 1:2]
     y[...] = (t0 * x4[...].astype(F32) + t1 * x0[...].astype(F32)).astype(BF)
+    z = out.at[192:384]
     gated_units(y, z, 192, (g_own, g_oth), 1024 * (9 - SPLIT), order)
     zv = z[...]
-    for r, s, cols in zip((r_own, r_oth), (s_own, s_oth), HALVES):
+    for r, cols in zip((r_own, r_oth), HALVES):
         out[0:192, cols] = (x0[:, cols].astype(F32) + dot(zv, rows_own_first(r.at[9], order))).astype(BF)
-        out[192:384, cols] = (skip[:, cols] + dot(zv, rows_own_first(s.at[9], order))).astype(BF)
-
-
-def skip_kernel(z, s_own, s_oth, out):
+
+
+def skip_kernel(z_own, z_oth, w, out):
     _, order = row_order()
-    for s, cols in zip((s_own, s_oth), HALVES):
-        total = dot(z[0], rows_own_first(s.at[0], order))
+    for z, at, rows in ((z_own, 0, order), (z_oth, 192, order[::-1])):
+        total = dot(z[0], rows_own_first(w.at[0], rows))
         for layer in range(1, 9):
-            total = total + dot(z[layer], rows_own_first(s.at[layer], order))
-        out[:, cols] = total
-
-
-def outputs_kernel(g, stream, skips, mixed):
+            total = total + dot(z[layer], rows_own_first(w.at[layer], rows))
+        out[at : at + 192] = total
+
+
+def outputs_kernel(g, skip, w, stream, skips, mixed):
     core = lax.axis_index("chan")
-    for half in range(2):
-
-        @pl.when(core == half)
-        def _(half=half):
-            for out, at in ((stream, 0), (skips, 192)):
-                for k in range(2):
-                    cols = HALVES[0 if k == half else 1]
-                    out[k] = g[k, at : at + 128, cols]
+    for me in range(2):
+
+        @pl.when(core == me)
+        def _(me=me):
+            weights = {k: rows_own_first(w.at[9], (256 * k, 256 - 256 * k)) for k in range(2)}
+
+            def fill(out, pieces):
+                for k, rows in enumerate(pieces):
+                    out[k] = rows[0:128].astype(BF)
                     for j in range(2):
-                        lanes = slice(cols.start + 128 * j, cols.start + 128 * j + 128)
-                        mixed[j, pl.ds(k, 64, stride=2)] = g[k, at + 128 : at + 192, lanes].astype(F32)
+                        mixed[j, pl.ds(k, 64, stride=2)] = rows[128:192, 128 * j : 128 * j + 128]
                 for j in range(2):
                     out[2, :, 128 * j : 128 * j + 128] = mixed[j].astype(BF)
+
+            fill(stream, [g[k, 0:192, HALVES[0 if k == me else 1]].astype(F32) for k in range(2)])
+            sums = (skip[0:192], skip[192:384])
+            fill(skips, [sums[0 if k == me else 1] + dot(g[k, 192:384], weights[k]) for k in range(2)])
 
 
 def call(body, inputs, outs, scratch, flops, spaces=None, vmem_mib=24):
@@ -235,13 +235,12 @@
     vm = pltpu.VMEM
     own = lax.all_gather(signal, "chan", axis=2, tiled=True)
     h1 = from_two(own, (1, 2))
-    h2 = from_two(own, (3, 4))
+    h2 = from_two(own, (4, 3))
     r_oth = other_core(w_res)
     ga_own = relayout(0, SPLIT, MIB_A, w_gate)
     ga_oth = other_core(ga_own)
     gb_own = relayout(SPLIT, 10 - SPLIT, MIB_B, w_gate, taps)
     gb_oth = other_core(gb_own)
-    s_oth = other_core(w_skip)
     h1 = lax.all_gather(h1, "chan", axis=0)
     h2 = lax.all_gather(h2, "chan", axis=0)
     x9, zs, taps_all = call(
@@ -258,16 +257,23 @@
         7000 * 512 * 1536 * 2,
     )
     x9_far = from_earlier(x9, 4)
-    skip = call(skip_kernel, [zs, w_skip, s_oth], sds((192, 512), F32), [], 9 * 192 * 512 * 512 * 2)
+    zs_oth = other_core(zs)
+    skip = call(skip_kernel, [zs, zs_oth, w_skip], sds((384, 256), F32), [], 9 * 192 * 512 * 512 * 2)
     both = call(
         last_layer,
-        [x9, x9_far, skip, taps_all, gb_own, gb_oth, w_res, r_oth, w_skip, s_oth],
+        [x9, x9_far, taps_all, gb_own, gb_oth, w_res, r_oth],
         sds((384, 512), BF),
-        [vm((192, 512), BF), vm((192, 512), BF)],
-        192 * 512 * 2048 * 2,
+        [vm((192, 512), BF)],
+        192 * 512 * 1536 * 2,
     )
     both = lax.all_gather(both, "chan", axis=0)
-    return call(outputs_kernel, [both], (sds((3, 128, 256), BF), sds((3, 128, 256), BF)), [vm((2, 128, 128), F32)], 1)
+    return call(
+        outputs_kernel,
+        [both, skip, w_skip],
+        (sds((3, 128, 256), BF), sds((3, 128, 256), BF)),
+        [vm((2, 128, 128), F32)],
+        384 * 512 * 256 * 2,
+    )
 
 
 def solution(mesh):

time: 90.8 us -> 85.1 us (0.937)
  blocking collectives: 26 us -> 16.9 us
  local copies, waits for them, and re-layouts: 0.03 us -> 3.23 us
  starting transfers between devices: 17.6 us -> 19.2 us
  waiting for transfers between devices: 25.3 us -> 24.3 us
    all_gather x1, blocking collectives: 9.51 us -> 2.36 us  [local(): h2 = lax.all_gather(h2, 'chan', axis=0)]
    unnamed x10 -> x12, local copies, waits for them, and re-layouts: 0.03 us -> 3.23 us
    ppermute x2, waiting for transfers between devices: 17 us -> 14.7 us  [from_two(): return lax.ppermute(value, ('tm', 'chan'), pairs)]
    all_gather x1, blocking collectives: 8.31 us -> 6.47 us  [local(): own = lax.all_gather(signal, 'chan', axis=2, tiled=True)]
    ppermute x1, waiting for transfers between devices: 8.26 us -> 9.6 us  [from_earlier(): lax.ppermute(value, 'tm', [(i, i + steps) for i in range(count - steps)])]
    ppermute x2, starting transfers between devices: 6.55 us -> 7.82 us  [from_two(): return lax.ppermute(value, ('tm', 'chan'), pairs)]
  transfers between devices with their start and end apart: 7 -> 7, of which waited for: 3 -> 3; matrix products, arithmetic and copies ran while one was open for 0% -> 0% of each run, Pallas kernels for 18% -> 4%
where the time goes in v3:
time: 85.1 us; the launch traced here: 84.6 us
  waiting for transfers between devices  24.3 us (29%)
  Pallas kernels  20.2 us (24%)
  starting transfers between devices  19.2 us (23%)
  blocking collectives  16.9 us (20%)
  local copies, waits for them, and re-layouts  3.23 us (4%)
    pallas_call x6, Pallas kernels, call(): pl.pallas_call(body, out_shape=outs, in_specs=[pl.BlockSpec(memory_space=...  20.2 us
    ppermute x2, waiting for transfers between devices, from_two(): return lax.ppermute(value, ('tm', 'chan'), pairs)  14.7 us
    ppermute x1, waiting for transfers between devices, from_earlier(): lax.ppermute(value, 'tm', [(i, i + steps) for i in range(count - steps)])  9.6 us
    ppermute x4, starting transfers between devices, other_core(): return lax.ppermute(value, 'chan', [(0, 1), (1, 0)])  9.44 us
    ppermute x2, starting transfers between devices, from_two(): return lax.ppermute(value, ('tm', 'chan'), pairs)  7.82 us
    all_gather x1, blocking collectives, local(): own = lax.all_gather(signal, 'chan', axis=2, tiled=True)  6.47 us
    all_gather x1, blocking collectives, local(): h1 = lax.all_gather(h1, 'chan', axis=0)  4.93 us
    unnamed x12, local copies, waits for them, and re-layouts  3.23 us
  transfers between devices with their start and end apart: 7, of which 3 were waited for; matrix products, arithmetic and copies ran while one was open for 0% of the time, Pallas kernels for 4%

profile of v3, /device:TPU:257, one launch (start us, length us, event | category | flops | bytes accessed | tf_op | source)
XLA Modules:
  0.0 84.6 jit_solution(687771883236575788)
XLA Ops:
  0.6 2.5 %copy-done = bf16[10,512,2,256]{3,2,1,0:T(2,128)(2,1)S(1)} copy-done((bf16[10,512,2,256]{3,2,1,0:T(2,128)(2,1)S(1)}, bf16[10,512,2,256]{3,2,1,0:T(2,128)(2,1)}, u32[]{:S(2)}) %copy-start) | copy-done | bytes 5242904
  3.1 0.7 copy-done.3
  3.8 1.8 %shard_map.69.gb_own.g_own = bf16[5216,256]{1,0:T(8,128)(2,1)S(1)} custom-call(f32[10,2,256]{2,1,0:T(2,128)S(1)} %copy-done.3, bf16[10,512,2,256]{3,2,1,0:T(2,128)(2,1)S(1)} %copy-done), custom_call_target="tpu_custom_call" | custom-call | flops 1000000 | bytes 5263360 | tf_op jit(solution)/shard_map/pallas_call | solution.py:190
  5.7 0.0 copy-start.2
  5.7 2.8 %collective-permute-start.3 = (bf16[5216,256]{1,0:T(8,128)(2,1)S(1)}, bf16[5216,256]{1,0:T(8,128)(2,1)S(1)}, u32[]{:S(2)}, u32[]{:S(2)}) collective-permute-start(bf16[5216,256]{1,0:T(8,128)(2,1)S(1)} %shard_map.69.gb_own.g_own), channel_id=1, source_target_pairs={{0,1},{1,0},{2,3},{3,2},{4,5},{5,4},{6,7},{7,6},{8,9},{9,8},{10,11... | collective-permute-start | bytes 8011784 | tf_op jit(solution)/shard_map/ppermute | solution.py:34
  8.5 2.6 %shard_map.68.ga_own = bf16[5120,256]{1,0:T(8,128)(2,1)S(1)} custom-call(bf16[10,512,2,256]{3,2,1,0:T(2,128)(2,1)} %refs_1_.1), custom_call_target="tpu_custom_call" | custom-call | flops 1000000 | bytes 5242880 | tf_op jit(solution)/shard_map/pallas_call | solution.py:190
  11.1 0.0 copy-start.4
  11.1 1.9 %collective-permute-start.2 = (bf16[5120,256]{1,0:T(8,128)(2,1)S(1)}, bf16[5120,256]{1,0:T(8,128)(2,1)S(1)}, u32[]{:S(2)}, u32[]{:S(2)}) collective-permute-start(bf16[5120,256]{1,0:T(8,128)(2,1)S(1)} %shard_map.68.ga_own), channel_id=1, source_target_pairs={{0,1},{1,0},{2,3},{3,2},{4,5},{5,4},{6,7},{7,6},{8,9},{9,8},{10,11... | collective-permute-start | bytes 7864328 | tf_op jit(solution)/shard_map/ppermute | solution.py:34
  13.1 2.4 %collective-permute-start.4 = (bf16[10,512,256]{2,1,0:T(8,128)(2,1)S(1)}, bf16[10,512,256]{2,1,0:T(8,128)(2,1)S(1)}, u32[]{:S(2)}, u32[]{:S(2)}) collective-permute-start(bf16[10,512,256]{2,1,0:T(8,128)(2,1)S(1)} %copy-done.2), channel_id=1, source_target_pairs={{0,1},{1,0},{2,3},{3,2},{4,5},{5,4},{6,7},{7,6},{8,9},{9,8},{10,11... | collective-permute-start | bytes 7864328 | tf_op jit(solution)/shard_map/ppermute | solution.py:34
  15.5 6.5 %all_gather.21.own = bf16[3,128,512]{2,1,0:T(8,128)(2,1)S(1)} all-gather(bf16[3,128,256]{2,1,0:T(8,128)(2,1)S(1)} %copy-done.5), channel_id=1, replica_groups=mesh['tm'=256,'chan'=2] {'chan'}, dimensions={2}, use_global_device_ids=true | all-gather | bytes 589824 | tf_op jit(solution)/shard_map/all_gather | solution.py:236
  22.0 4.4 %collective-permute-start.1 = (bf16[3,128,512]{2,1,0:T(8,128)(2,1)S(1)}, bf16[3,128,512]{2,1,0:T(8,128)(2,1)S(1)}, u32[]{:S(2)}, u32[]{:S(2)}) collective-permute-start(bf16[3,128,512]{2,1,0:T(8,128)(2,1)S(1)} %all_gather.21.own), channel_id=1, source_target_pairs={{0,8},{2,10},{4,12},{6,14},{8,16},{10,18},{12,20},{14,22},{16,24},... | collective-permute-start | bytes 1179656 | tf_op jit(solution)/shard_map/ppermute | solution.py:30
  26.3 3.4 %collective-permute-start = (bf16[3,128,512]{2,1,0:T(8,128)(2,1)S(1)}, bf16[3,128,512]{2,1,0:T(8,128)(2,1)S(1)}, u32[]{:S(2)}, u32[]{:S(2)}) collective-permute-start(bf16[3,128,512]{2,1,0:T(8,128)(2,1)S(1)} %all_gather.21.own), channel_id=1, source_target_pairs={{0,2},{2,4},{4,6},{6,8},{8,10},{10,12},{12,14},{14,16},{16,18},{18... | collective-permute-start | bytes 1179656 | tf_op jit(solution)/shard_map/ppermute | solution.py:30
  29.8 8.5 %collective-permute-done.1 = bf16[3,128,512]{2,1,0:T(8,128)(2,1)S(1)} collective-permute-done((bf16[3,128,512]{2,1,0:T(8,128)(2,1)S(1)}, bf16[3,128,512]{2,1,0:T(8,128)(2,1)S(1)}, u32[]{:S(2)}, u32[]{:S(2)}) %collective-permute-start.1) | collective-permute-done | bytes 393248 | tf_op jit(solution)/shard_map/ppermute | solution.py:30
  38.3 2.4 %all-gather.1 = bf16[6,128,512]{2,1,0:T(8,128)(2,1)S(1)} all-gather(bf16[3,128,512]{2,1,0:T(8,128)(2,1)S(1)} %collective-permute-done.1), channel_id=3, replica_groups=mesh['tm'=256,'chan'=2] {'chan'}, dimensions={0}, use_global_device_ids=true | all-gather | bytes 1179648 | tf_op jit(solution)/shard_map/all_gather | solution.py:245
  40.6 6.2 %collective-permute-done = bf16[3,128,512]{2,1,0:T(8,128)(2,1)S(1)} collective-permute-done((bf16[3,128,512]{2,1,0:T(8,128)(2,1)S(1)}, bf16[3,128,512]{2,1,0:T(8,128)(2,1)S(1)}, u32[]{:S(2)}, u32[]{:S(2)}) %collective-permute-start) | collective-permute-done | bytes 393248 | tf_op jit(solution)/shard_map/ppermute | solution.py:30
  46.8 4.9 %all-gather = bf16[6,128,512]{2,1,0:T(8,128)(2,1)S(1)} all-gather(bf16[3,128,512]{2,1,0:T(8,128)(2,1)S(1)} %collective-permute-done), channel_id=2, replica_groups=mesh['tm'=256,'chan'=2] {'chan'}, dimensions={0}, use_global_device_ids=true | all-gather | bytes 1179648 | tf_op jit(solution)/shard_map/all_gather | solution.py:244
  51.8 13.2 %shard_map.70 = (bf16[192,512]{1,0:T(8,128)(2,1)S(1)}, bf16[9,192,512]{2,1,0:T(8,128)(2,1)S(1)}, f32[10,2,512]{2,1,0:T(2,128)S(1)}) custom-call(bf16[3,128,512]{2,1,0:T(8,128)(2,1)S(1)} %all_gather.21.own, bf16[2,3,128,512]{3,2,1,0:T(8,128)(2,1)S(1)} %bitcast.5, bf16[2,3,128,512]{3,2,1,0:T(8,128)(2,1)S(1)} %bitcast.4, f32[10,2,256]{2,1,0:T(2,128)S(1)} %copy-done.4, ...), custom_call_target="tpu_custom_call" | custom-call | flops 11010048000 | bytes 17813504 | tf_op jit(solution)/shard_map/pallas_call | solution.py:190
  65.0 2.3 %collective-permute-start.6 = (bf16[9,192,512]{2,1,0:T(8,128)(2,1)S(1)}, bf16[9,192,512]{2,1,0:T(8,128)(2,1)S(1)}, u32[]{:S(2)}, u32[]{:S(2)}) collective-permute-start(bf16[9,192,512]{2,1,0:T(8,128)(2,1)S(1)} %get-tuple-element.7.z_own), channel_id=1, source_target_pairs={{0,1},{1,0},{2,3},{3,2},{4,5},{5,4},{6,7},{7,6},{8,9},{9,8},{10,11... | collective-permute-start | bytes 5308424 | tf_op jit(solution)/shard_map/ppermute | solution.py:34
  67.2 1.9 %collective-permute-start.5 = (bf16[192,512]{1,0:T(8,128)(2,1)S(1)}, bf16[192,512]{1,0:T(8,128)(2,1)S(1)}, u32[]{:S(2)}, u32[]{:S(2)}) collective-permute-start(bf16[192,512]{1,0:T(8,128)(2,1)S(1)} %get-tuple-element.5.x0), channel_id=1, source_target_pairs={{0,8},{2,10},{4,12},{6,14},{8,16},{10,18},{12,20},{14,22},{16,24},... | collective-permute-start | bytes 589832 | tf_op jit(solution)/shard_map/ppermute | solution.py:24
  69.2 9.6 %collective-permute-done.5.x4 = bf16[192,512]{1,0:T(8,128)(2,1)S(1)} collective-permute-done((bf16[192,512]{1,0:T(8,128)(2,1)S(1)}, bf16[192,512]{1,0:T(8,128)(2,1)S(1)}, u32[]{:S(2)}, u32[]{:S(2)}) %collective-permute-start.5) | collective-permute-done | bytes 196640 | tf_op jit(solution)/shard_map/ppermute | solution.py:24
  78.8 0.5 shard_map.71
  79.3 3.1 %all-gather.2 = bf16[768,512]{1,0:T(8,128)(2,1)S(1)} all-gather(bf16[384,512]{1,0:T(8,128)(2,1)S(1)} %shard_map.71), channel_id=4, replica_groups=mesh['tm'=256,'chan'=2] {'chan'}, dimensions={0}, use_global_device_ids=true | all-gather | bytes 1179648 | tf_op jit(solution)/shard_map/all_gather | solution.py:269
  82.4 1.1 %shard_map.72.skip = f32[384,256]{1,0:T(8,128)S(1)} custom-call(bf16[9,192,512]{2,1,0:T(8,128)(2,1)S(1)} %get-tuple-element.7.z_own, bf16[9,192,512]{2,1,0:T(8,128)(2,1)S(1)} %collective-permute-done.6.z_oth, bf16[10,512,256]{2,1,0:T(8,128)(2,1)S(1)} %copy-done.1), custom_call_target="tpu_custom_call" | custom-call | flops 905969664 | bytes 6160384 | tf_op jit(solution)/shard_map/pallas_call | solution.py:190
  83.6 1.1 %shard_map.73 = (bf16[3,128,256]{2,1,0:T(8,128)(2,1)}, bf16[3,128,256]{2,1,0:T(8,128)(2,1)}) custom-call(bf16[2,384,512]{2,1,0:T(8,128)(2,1)S(1)} %bitcast.3, f32[384,256]{1,0:T(8,128)S(1)} %shard_map.72.skip, bf16[10,512,256]{2,1,0:T(8,128)(2,1)S(1)} %copy-done.1), custom_call_target="tpu_custom_call" | custom-call | flops 100663296 | bytes 3801088 | tf_op jit(solution)/shard_map/pallas_call | solution.py:190
  (12 shorter events, 0.0 us)
Async XLA Ops:
  0.6 2.5 %copy-start = (bf16[10,512,2,256]{3,2,1,0:T(2,128)(2,1)S(1)}, bf16[10,512,2,256]{3,2,1,0:T(2,128)(2,1)}, u32[]{:S(2)}) copy-start(bf16[10,512,2,256]{3,2,1,0:T(2,128)(2,1)} %refs_1_.1) | copy-start | bytes 15728644
  3.1 0.7 copy-start.3
  5.7 7.4 %copy-start.2 = (bf16[10,512,256]{2,1,0:T(8,128)(2,1)S(1)}, bf16[10,512,256]{2,1,0:T(8,128)(2,1)}, u32[]{:S(2)}) copy-start(bf16[10,512,256]{2,1,0:T(8,128)(2,1)} %r_own.3) | copy-start | bytes 7864324
  5.7 9.8 %copy-start.5 = (bf16[3,128,256]{2,1,0:T(8,128)(2,1)S(1)}, bf16[3,128,256]{2,1,0:T(8,128)(2,1)}, u32[]{:S(2)}) copy-start(bf16[3,128,256]{2,1,0:T(8,128)(2,1)} %param.5) | copy-start | bytes 589828
  5.7 46.1 %collective-permute-start.3 = (bf16[5216,256]{1,0:T(8,128)(2,1)S(1)}, bf16[5216,256]{1,0:T(8,128)(2,1)S(1)}, u32[]{:S(2)}, u32[]{:S(2)}) collective-permute-start(bf16[5216,256]{1,0:T(8,128)(2,1)S(1)} %shard_map.69.gb_own.g_own), channel_id=1, source_target_pairs={{0,1},{1,0},{2,3},{3,2},{4,5},{5,4},{6,7},{7,6},{8,9},{9,8},{10,11... | collective-permute-start | bytes 8011784 | tf_op jit(solution)/shard_map/ppermute | solution.py:34
  11.1 40.6 %copy-start.4 = (f32[10,2,256]{2,1,0:T(2,128)S(1)}, f32[10,2,256]{2,1,0:T(2,128)}, u32[]{:S(2)}) copy-start(f32[10,2,256]{2,1,0:T(2,128)} %t_own.1) | copy-start | bytes 61444
  11.1 40.6 %collective-permute-start.2 = (bf16[5120,256]{1,0:T(8,128)(2,1)S(1)}, bf16[5120,256]{1,0:T(8,128)(2,1)S(1)}, u32[]{:S(2)}, u32[]{:S(2)}) collective-permute-start(bf16[5120,256]{1,0:T(8,128)(2,1)S(1)} %shard_map.68.ga_own), channel_id=1, source_target_pairs={{0,1},{1,0},{2,3},{3,2},{4,5},{5,4},{6,7},{7,6},{8,9},{9,8},{10,11... | collective-permute-start | bytes 7864328 | tf_op jit(solution)/shard_map/ppermute | solution.py:34
  13.1 38.7 %collective-permute-start.4 = (bf16[10,512,256]{2,1,0:T(8,128)(2,1)S(1)}, bf16[10,512,256]{2,1,0:T(8,128)(2,1)S(1)}, u32[]{:S(2)}, u32[]{:S(2)}) collective-permute-start(bf16[10,512,256]{2,1,0:T(8,128)(2,1)S(1)} %copy-done.2), channel_id=1, source_target_pairs={{0,1},{1,0},{2,3},{3,2},{4,5},{5,4},{6,7},{7,6},{8,9},{9,8},{10,11... | collective-permute-start | bytes 7864328 | tf_op jit(solution)/shard_map/ppermute | solution.py:34
  22.0 16.3 %collective-permute-start.1 = (bf16[3,128,512]{2,1,0:T(8,128)(2,1)S(1)}, bf16[3,128,512]{2,1,0:T(8,128)(2,1)S(1)}, u32[]{:S(2)}, u32[]{:S(2)}) collective-permute-start(bf16[3,128,512]{2,1,0:T(8,128)(2,1)S(1)} %all_gather.21.own), channel_id=1, source_target_pairs={{0,8},{2,10},{4,12},{6,14},{8,16},{10,18},{12,20},{14,22},{16,24},... | collective-permute-start | bytes 1179656 | tf_op jit(solution)/shard_map/ppermute | solution.py:30
  26.3 20.5 %collective-permute-start = (bf16[3,128,512]{2,1,0:T(8,128)(2,1)S(1)}, bf16[3,128,512]{2,1,0:T(8,128)(2,1)S(1)}, u32[]{:S(2)}, u32[]{:S(2)}) collective-permute-start(bf16[3,128,512]{2,1,0:T(8,128)(2,1)S(1)} %all_gather.21.own), channel_id=1, source_target_pairs={{0,2},{2,4},{4,6},{6,8},{8,10},{10,12},{12,14},{14,16},{16,18},{18... | collective-permute-start | bytes 1179656 | tf_op jit(solution)/shard_map/ppermute | solution.py:30
  65.0 17.5 %collective-permute-start.6 = (bf16[9,192,512]{2,1,0:T(8,128)(2,1)S(1)}, bf16[9,192,512]{2,1,0:T(8,128)(2,1)S(1)}, u32[]{:S(2)}, u32[]{:S(2)}) collective-permute-start(bf16[9,192,512]{2,1,0:T(8,128)(2,1)S(1)} %get-tuple-element.7.z_own), channel_id=1, source_target_pairs={{0,1},{1,0},{2,3},{3,2},{4,5},{5,4},{6,7},{7,6},{8,9},{9,8},{10,11... | collective-permute-start | bytes 5308424 | tf_op jit(solution)/shard_map/ppermute | solution.py:34
  67.2 11.5 %collective-permute-start.5 = (bf16[192,512]{1,0:T(8,128)(2,1)S(1)}, bf16[192,512]{1,0:T(8,128)(2,1)S(1)}, u32[]{:S(2)}, u32[]{:S(2)}) collective-permute-start(bf16[192,512]{1,0:T(8,128)(2,1)S(1)} %get-tuple-element.5.x0), channel_id=1, source_target_pairs={{0,8},{2,10},{4,12},{6,14},{8,16},{10,18},{12,20},{14,22},{16,24},... | collective-permute-start | bytes 589832 | tf_op jit(solution)/shard_map/ppermute | solution.py:24
  78.8 3.7 %copy-start.1 = (bf16[10,512,256]{2,1,0:T(8,128)(2,1)S(1)}, bf16[10,512,256]{2,1,0:T(8,128)(2,1)}, u32[]{:S(2)}) copy-start(bf16[10,512,256]{2,1,0:T(8,128)(2,1)} %w.3) | copy-start | bytes 7864324

commit v4 on v3

--- a/solution.py
+++ b/solution.py
@@ -70,7 +70,7 @@
     xa[0:PAD] = zero
     xb[:, 0:PAD] = jnp.zeros((4, PAD, 128), F32)
     xp[0:PAD] = zero
-    blocks = ((h2, 0), (h2, 1), (h1, 1), (h1, 0))
+    blocks = ((h2, 0), (h2, 1), (h1, 0), (h1, 1))
 
     def load(rows, source):
         for start, cols in zip(order, HALVES):
@@ -175,11 +175,11 @@
                 for k, rows in enumerate(pieces):
                     out[k] = rows[0:128].astype(BF)
                     for j in range(2):
-                        mixed[j, pl.ds(k, 64, stride=2)] = rows[128:192, 128 * j : 128 * j + 128]
+                        mixed[j, pl.ds(k, 64, stride=2)] = rows[128:192, 128 * j : 128 * j + 128].astype(F32)
                 for j in range(2):
                     out[2, :, 128 * j : 128 * j + 128] = mixed[j].astype(BF)
 
-            fill(stream, [g[k, 0:192, HALVES[0 if k == me else 1]].astype(F32) for k in range(2)])
+            fill(stream, [g[k, 0:192, HALVES[0 if k == me else 1]] for k in range(2)])
             sums = (skip[0:192], skip[192:384])
             fill(skips, [sums[0 if k == me else 1] + dot(g[k, 192:384], weights[k]) for k in range(2)])
 
@@ -234,7 +234,7 @@
     sds = jax.ShapeDtypeStruct
     vm = pltpu.VMEM
     own = lax.all_gather(signal, "chan", axis=2, tiled=True)
-    h1 = from_two(own, (1, 2))
+    h1 = from_two(own, (2, 1))
     h2 = from_two(own, (4, 3))
     r_oth = other_core(w_res)
     ga_own = relayout(0, SPLIT, MIB_A, w_gate)

time: 85.1 us -> 84.5 us (level)
  the two profiles are of different devices: /device:TPU:257 before, /device:TPU:259 now
where the time goes in v4:
time: 84.5 us; the launch traced here: 84 us
  blocking collectives  22.4 us (27%)
  Pallas kernels  20.2 us (24%)
  waiting for transfers between devices  19.6 us (23%)
  starting transfers between devices  17.6 us (21%)
  local copies, waits for them, and re-layouts  3.23 us (4%)
    pallas_call x6, Pallas kernels, call(): pl.pallas_call(body, out_shape=outs, in_specs=[pl.BlockSpec(memory_space=...  20.2 us
    all_gather x1, blocking collectives, local(): h1 = lax.all_gather(h1, 'chan', axis=0)  10.5 us
    ppermute x2, waiting for transfers between devices, from_two(): return lax.ppermute(value, ('tm', 'chan'), pairs)  10 us
    ppermute x1, waiting for transfers between devices, from_earlier(): lax.ppermute(value, 'tm', [(i, i + steps) for i in range(count - steps)])  9.6 us
    ppermute x4, starting transfers between devices, other_core(): return lax.ppermute(value, 'chan', [(0, 1), (1, 0)])  9.44 us
    all_gather x1, blocking collectives, local(): own = lax.all_gather(signal, 'chan', axis=2, tiled=True)  6.47 us
    ppermute x2, starting transfers between devices, from_two(): return lax.ppermute(value, ('tm', 'chan'), pairs)  6.28 us
    unnamed x12, local copies, waits for them, and re-layouts  3.23 us
  transfers between devices with their start and end apart: 7, of which 2 were waited for; matrix products, arithmetic and copies ran while one was open for 0% of the time, Pallas kernels for 4%

profile of v4, /device:TPU:259, one launch (start us, length us, event | category | flops | bytes accessed | tf_op | source)
XLA Modules:
  0.0 84.0 jit_solution(1774197072027989998)
XLA Ops:
  0.6 0.0 copy-start
  0.6 2.5 %copy-done = bf16[10,512,2,256]{3,2,1,0:T(2,128)(2,1)S(1)} copy-done((bf16[10,512,2,256]{3,2,1,0:T(2,128)(2,1)S(1)}, bf16[10,512,2,256]{3,2,1,0:T(2,128)(2,1)}, u32[]{:S(2)}) %copy-start) | copy-done | bytes 5242904
  3.1 0.7 copy-done.3
  3.8 1.8 %shard_map.69.gb_own.g_own = bf16[5216,256]{1,0:T(8,128)(2,1)S(1)} custom-call(f32[10,2,256]{2,1,0:T(2,128)S(1)} %copy-done.3, bf16[10,512,2,256]{3,2,1,0:T(2,128)(2,1)S(1)} %copy-done), custom_call_target="tpu_custom_call" | custom-call | flops 1000000 | bytes 5263360 | tf_op jit(solution)/shard_map/pallas_call | solution.py:190
  5.7 0.0 copy-start.2
  5.7 0.0 copy-start.5
  5.7 2.8 %collective-permute-start.3 = (bf16[5216,256]{1,0:T(8,128)(2,1)S(1)}, bf16[5216,256]{1,0:T(8,128)(2,1)S(1)}, u32[]{:S(2)}, u32[]{:S(2)}) collective-permute-start(bf16[5216,256]{1,0:T(8,128)(2,1)S(1)} %shard_map.69.gb_own.g_own), channel_id=1, source_target_pairs={{0,1},{1,0},{2,3},{3,2},{4,5},{5,4},{6,7},{7,6},{8,9},{9,8},{10,11... | collective-permute-start | bytes 8011784 | tf_op jit(solution)/shard_map/ppermute | solution.py:34
  8.5 2.6 %shard_map.68.ga_own = bf16[5120,256]{1,0:T(8,128)(2,1)S(1)} custom-call(bf16[10,512,2,256]{3,2,1,0:T(2,128)(2,1)} %refs_1_.1), custom_call_target="tpu_custom_call" | custom-call | flops 1000000 | bytes 5242880 | tf_op jit(solution)/shard_map/pallas_call | solution.py:190
  11.1 1.9 %collective-permute-start.2 = (bf16[5120,256]{1,0:T(8,128)(2,1)S(1)}, bf16[5120,256]{1,0:T(8,128)(2,1)S(1)}, u32[]{:S(2)}, u32[]{:S(2)}) collective-permute-start(bf16[5120,256]{1,0:T(8,128)(2,1)S(1)} %shard_map.68.ga_own), channel_id=1, source_target_pairs={{0,1},{1,0},{2,3},{3,2},{4,5},{5,4},{6,7},{7,6},{8,9},{9,8},{10,11... | collective-permute-start | bytes 7864328 | tf_op jit(solution)/shard_map/ppermute | solution.py:34
  13.1 2.4 %collective-permute-start.4 = (bf16[10,512,256]{2,1,0:T(8,128)(2,1)S(1)}, bf16[10,512,256]{2,1,0:T(8,128)(2,1)S(1)}, u32[]{:S(2)}, u32[]{:S(2)}) collective-permute-start(bf16[10,512,256]{2,1,0:T(8,128)(2,1)S(1)} %copy-done.2), channel_id=1, source_target_pairs={{0,1},{1,0},{2,3},{3,2},{4,5},{5,4},{6,7},{7,6},{8,9},{9,8},{10,11... | collective-permute-start | bytes 7864328 | tf_op jit(solution)/shard_map/ppermute | solution.py:34
  15.5 6.5 %all_gather.21.own = bf16[3,128,512]{2,1,0:T(8,128)(2,1)S(1)} all-gather(bf16[3,128,256]{2,1,0:T(8,128)(2,1)S(1)} %copy-done.5), channel_id=1, replica_groups=mesh['tm'=256,'chan'=2] {'chan'}, dimensions={2}, use_global_device_ids=true | all-gather | bytes 589824 | tf_op jit(solution)/shard_map/all_gather | solution.py:236
  22.0 3.2 %collective-permute-start.1 = (bf16[3,128,512]{2,1,0:T(8,128)(2,1)S(1)}, bf16[3,128,512]{2,1,0:T(8,128)(2,1)S(1)}, u32[]{:S(2)}, u32[]{:S(2)}) collective-permute-start(bf16[3,128,512]{2,1,0:T(8,128)(2,1)S(1)} %all_gather.21.own), channel_id=1, source_target_pairs={{0,8},{2,10},{4,12},{6,14},{8,16},{10,18},{12,20},{14,22},{16,24},... | collective-permute-start | bytes 1179656 | tf_op jit(solution)/shard_map/ppermute | solution.py:30
  25.1 3.1 %collective-permute-start = (bf16[3,128,512]{2,1,0:T(8,128)(2,1)S(1)}, bf16[3,128,512]{2,1,0:T(8,128)(2,1)S(1)}, u32[]{:S(2)}, u32[]{:S(2)}) collective-permute-start(bf16[3,128,512]{2,1,0:T(8,128)(2,1)S(1)} %all_gather.21.own), channel_id=1, source_target_pairs={{0,4},{2,6},{4,8},{6,10},{8,12},{10,14},{12,16},{14,18},{16,20},{1... | collective-permute-start | bytes 1179656 | tf_op jit(solution)/shard_map/ppermute | solution.py:30
  28.3 10.0 %collective-permute-done.1 = bf16[3,128,512]{2,1,0:T(8,128)(2,1)S(1)} collective-permute-done((bf16[3,128,512]{2,1,0:T(8,128)(2,1)S(1)}, bf16[3,128,512]{2,1,0:T(8,128)(2,1)S(1)}, u32[]{:S(2)}, u32[]{:S(2)}) %collective-permute-start.1) | collective-permute-done | bytes 393248 | tf_op jit(solution)/shard_map/ppermute | solution.py:30
  38.3 2.4 %all-gather.1 = bf16[6,128,512]{2,1,0:T(8,128)(2,1)S(1)} all-gather(bf16[3,128,512]{2,1,0:T(8,128)(2,1)S(1)} %collective-permute-done.1), channel_id=3, replica_groups=mesh['tm'=256,'chan'=2] {'chan'}, dimensions={0}, use_global_device_ids=true | all-gather | bytes 1179648 | tf_op jit(solution)/shard_map/all_gather | solution.py:245
  40.6 10.5 %all-gather = bf16[6,128,512]{2,1,0:T(8,128)(2,1)S(1)} all-gather(bf16[3,128,512]{2,1,0:T(8,128)(2,1)S(1)} %collective-permute-done), channel_id=2, replica_groups=mesh['tm'=256,'chan'=2] {'chan'}, dimensions={0}, use_global_device_ids=true | all-gather | bytes 1179648 | tf_op jit(solution)/shard_map/all_gather | solution.py:244
  51.1 13.2 %shard_map.70 = (bf16[192,512]{1,0:T(8,128)(2,1)S(1)}, bf16[9,192,512]{2,1,0:T(8,128)(2,1)S(1)}, f32[10,2,512]{2,1,0:T(2,128)S(1)}) custom-call(bf16[3,128,512]{2,1,0:T(8,128)(2,1)S(1)} %all_gather.21.own, bf16[2,3,128,512]{3,2,1,0:T(8,128)(2,1)S(1)} %bitcast.5, bf16[2,3,128,512]{3,2,1,0:T(8,128)(2,1)S(1)} %bitcast.4, f32[10,2,256]{2,1,0:T(2,128)S(1)} %copy-done.4, ...), custom_call_target="tpu_custom_call" | custom-call | flops 11010048000 | bytes 17813504 | tf_op jit(solution)/shard_map/pallas_call | solution.py:190
  64.3 2.3 %collective-permute-start.6 = (bf16[9,192,512]{2,1,0:T(8,128)(2,1)S(1)}, bf16[9,192,512]{2,1,0:T(8,128)(2,1)S(1)}, u32[]{:S(2)}, u32[]{:S(2)}) collective-permute-start(bf16[9,192,512]{2,1,0:T(8,128)(2,1)S(1)} %get-tuple-element.7.z_own), channel_id=1, source_target_pairs={{0,1},{1,0},{2,3},{3,2},{4,5},{5,4},{6,7},{7,6},{8,9},{9,8},{10,11... | collective-permute-start | bytes 5308424 | tf_op jit(solution)/shard_map/ppermute | solution.py:34
  66.6 1.9 %collective-permute-start.5 = (bf16[192,512]{1,0:T(8,128)(2,1)S(1)}, bf16[192,512]{1,0:T(8,128)(2,1)S(1)}, u32[]{:S(2)}, u32[]{:S(2)}) collective-permute-start(bf16[192,512]{1,0:T(8,128)(2,1)S(1)} %get-tuple-element.5.x0), channel_id=1, source_target_pairs={{0,8},{2,10},{4,12},{6,14},{8,16},{10,18},{12,20},{14,22},{16,24},... | collective-permute-start | bytes 589832 | tf_op jit(solution)/shard_map/ppermute | solution.py:24
  68.5 9.6 %collective-permute-done.5.x4 = bf16[192,512]{1,0:T(8,128)(2,1)S(1)} collective-permute-done((bf16[192,512]{1,0:T(8,128)(2,1)S(1)}, bf16[192,512]{1,0:T(8,128)(2,1)S(1)}, u32[]{:S(2)}, u32[]{:S(2)}) %collective-permute-start.5) | collective-permute-done | bytes 196640 | tf_op jit(solution)/shard_map/ppermute | solution.py:24
  78.1 0.5 shard_map.71
  78.7 3.1 %all-gather.2 = bf16[768,512]{1,0:T(8,128)(2,1)S(1)} all-gather(bf16[384,512]{1,0:T(8,128)(2,1)S(1)} %shard_map.71), channel_id=4, replica_groups=mesh['tm'=256,'chan'=2] {'chan'}, dimensions={0}, use_global_device_ids=true | all-gather | bytes 1179648 | tf_op jit(solution)/shard_map/all_gather | solution.py:269
  81.8 1.1 %shard_map.72.skip = f32[384,256]{1,0:T(8,128)S(1)} custom-call(bf16[9,192,512]{2,1,0:T(8,128)(2,1)S(1)} %get-tuple-element.7.z_own, bf16[9,192,512]{2,1,0:T(8,128)(2,1)S(1)} %collective-permute-done.6.z_oth, bf16[10,512,256]{2,1,0:T(8,128)(2,1)S(1)} %copy-done.1), custom_call_target="tpu_custom_call" | custom-call | flops 905969664 | bytes 6160384 | tf_op jit(solution)/shard_map/pallas_call | solution.py:190
  82.9 1.1 %shard_map.73 = (bf16[3,128,256]{2,1,0:T(8,128)(2,1)}, bf16[3,128,256]{2,1,0:T(8,128)(2,1)}) custom-call(bf16[2,384,512]{2,1,0:T(8,128)(2,1)S(1)} %bitcast.3, f32[384,256]{1,0:T(8,128)S(1)} %shard_map.72.skip, bf16[10,512,256]{2,1,0:T(8,128)(2,1)S(1)} %copy-done.1), custom_call_target="tpu_custom_call" | custom-call | flops 100663296 | bytes 3801088 | tf_op jit(solution)/shard_map/pallas_call | solution.py:190
  (12 shorter events, 0.0 us)
Async XLA Ops:
  0.6 2.5 %copy-start = (bf16[10,512,2,256]{3,2,1,0:T(2,128)(2,1)S(1)}, bf16[10,512,2,256]{3,2,1,0:T(2,128)(2,1)}, u32[]{:S(2)}) copy-start(bf16[10,512,2,256]{3,2,1,0:T(2,128)(2,1)} %refs_1_.1) | copy-start | bytes 15728644
  3.1 0.7 copy-start.3
  5.7 7.4 %copy-start.2 = (bf16[10,512,256]{2,1,0:T(8,128)(2,1)S(1)}, bf16[10,512,256]{2,1,0:T(8,128)(2,1)}, u32[]{:S(2)}) copy-start(bf16[10,512,256]{2,1,0:T(8,128)(2,1)} %r_own.3) | copy-start | bytes 7864324
  5.7 9.8 %copy-start.5 = (bf16[3,128,256]{2,1,0:T(8,128)(2,1)S(1)}, bf16[3,128,256]{2,1,0:T(8,128)(2,1)}, u32[]{:S(2)}) copy-start(bf16[3,128,256]{2,1,0:T(8,128)(2,1)} %param.5) | copy-start | bytes 589828
  5.7 45.4 %collective-permute-start.3 = (bf16[5216,256]{1,0:T(8,128)(2,1)S(1)}, bf16[5216,256]{1,0:T(8,128)(2,1)S(1)}, u32[]{:S(2)}, u32[]{:S(2)}) collective-permute-start(bf16[5216,256]{1,0:T(8,128)(2,1)S(1)} %shard_map.69.gb_own.g_own), channel_id=1, source_target_pairs={{0,1},{1,0},{2,3},{3,2},{4,5},{5,4},{6,7},{7,6},{8,9},{9,8},{10,11... | collective-permute-start | bytes 8011784 | tf_op jit(solution)/shard_map/ppermute | solution.py:34
  11.1 40.0 %copy-start.4 = (f32[10,2,256]{2,1,0:T(2,128)S(1)}, f32[10,2,256]{2,1,0:T(2,128)}, u32[]{:S(2)}) copy-start(f32[10,2,256]{2,1,0:T(2,128)} %t_own.1) | copy-start | bytes 61444
  11.1 40.0 %collective-permute-start.2 = (bf16[5120,256]{1,0:T(8,128)(2,1)S(1)}, bf16[5120,256]{1,0:T(8,128)(2,1)S(1)}, u32[]{:S(2)}, u32[]{:S(2)}) collective-permute-start(bf16[5120,256]{1,0:T(8,128)(2,1)S(1)} %shard_map.68.ga_own), channel_id=1, source_target_pairs={{0,1},{1,0},{2,3},{3,2},{4,5},{5,4},{6,7},{7,6},{8,9},{9,8},{10,11... | collective-permute-start | bytes 7864328 | tf_op jit(solution)/shard_map/ppermute | solution.py:34
  13.1 38.1 %collective-permute-start.4 = (bf16[10,512,256]{2,1,0:T(8,128)(2,1)S(1)}, bf16[10,512,256]{2,1,0:T(8,128)(2,1)S(1)}, u32[]{:S(2)}, u32[]{:S(2)}) collective-permute-start(bf16[10,512,256]{2,1,0:T(8,128)(2,1)S(1)} %copy-done.2), channel_id=1, source_target_pairs={{0,1},{1,0},{2,3},{3,2},{4,5},{5,4},{6,7},{7,6},{8,9},{9,8},{10,11... | collective-permute-start | bytes 7864328 | tf_op jit(solution)/shard_map/ppermute | solution.py:34
  22.0 16.3 %collective-permute-start.1 = (bf16[3,128,512]{2,1,0:T(8,128)(2,1)S(1)}, bf16[3,128,512]{2,1,0:T(8,128)(2,1)S(1)}, u32[]{:S(2)}, u32[]{:S(2)}) collective-permute-start(bf16[3,128,512]{2,1,0:T(8,128)(2,1)S(1)} %all_gather.21.own), channel_id=1, source_target_pairs={{0,8},{2,10},{4,12},{6,14},{8,16},{10,18},{12,20},{14,22},{16,24},... | collective-permute-start | bytes 1179656 | tf_op jit(solution)/shard_map/ppermute | solution.py:30
  25.1 15.5 %collective-permute-start = (bf16[3,128,512]{2,1,0:T(8,128)(2,1)S(1)}, bf16[3,128,512]{2,1,0:T(8,128)(2,1)S(1)}, u32[]{:S(2)}, u32[]{:S(2)}) collective-permute-start(bf16[3,128,512]{2,1,0:T(8,128)(2,1)S(1)} %all_gather.21.own), channel_id=1, source_target_pairs={{0,4},{2,6},{4,8},{6,10},{8,12},{10,14},{12,16},{14,18},{16,20},{1... | collective-permute-start | bytes 1179656 | tf_op jit(solution)/shard_map/ppermute | solution.py:30
  64.3 17.5 %collective-permute-start.6 = (bf16[9,192,512]{2,1,0:T(8,128)(2,1)S(1)}, bf16[9,192,512]{2,1,0:T(8,128)(2,1)S(1)}, u32[]{:S(2)}, u32[]{:S(2)}) collective-permute-start(bf16[9,192,512]{2,1,0:T(8,128)(2,1)S(1)} %get-tuple-element.7.z_own), channel_id=1, source_target_pairs={{0,1},{1,0},{2,3},{3,2},{4,5},{5,4},{6,7},{7,6},{8,9},{9,8},{10,11... | collective-permute-start | bytes 5308424 | tf_op jit(solution)/shard_map/ppermute | solution.py:34
  66.6 11.5 %collective-permute-start.5 = (bf16[192,512]{1,0:T(8,128)(2,1)S(1)}, bf16[192,512]{1,0:T(8,128)(2,1)S(1)}, u32[]{:S(2)}, u32[]{:S(2)}) collective-permute-start(bf16[192,512]{1,0:T(8,128)(2,1)S(1)} %get-tuple-element.5.x0), channel_id=1, source_target_pairs={{0,8},{2,10},{4,12},{6,14},{8,16},{10,18},{12,20},{14,22},{16,24},... | collective-permute-start | bytes 589832 | tf_op jit(solution)/shard_map/ppermute | solution.py:24
  78.1 3.7 %copy-start.1 = (bf16[10,512,256]{2,1,0:T(8,128)(2,1)S(1)}, bf16[10,512,256]{2,1,0:T(8,128)(2,1)}, u32[]{:S(2)}) copy-start(bf16[10,512,256]{2,1,0:T(8,128)(2,1)} %w.3) | copy-start | bytes 7864324
